TPU v7x, 128 devices: a whole 4x4x4 slice. The times are simulated.
128 devices in a mesh: row: 8 (over x_hi, z), col: 16 (over x_lo, y, core).
Axes of the slice: x: 4 (x_hi: 2, x_lo: 2; x = x_hi * 2 + x_lo), y: 4, z: 4, core: 2. Of those that a mesh axis runs over, the one named last changes fastest.
Arguments:
- tokens: bfloat16 [1024, 12288], P('row', 'col'), may hold values from -6 to 6
- prev_tokens: bfloat16 [1024, 12288], P('row', 'col'), may hold values from -6 to 6
- hidden_grad: bfloat16 [1024, 49152], P('col', 'row'), may hold values from -6 to 6
- active_blocks: int32 [1], replicated, may hold values from 6 to 16
- weight: bfloat16 [12288, 49152], P('col', 'row'), may hold values from -0.0546875 to 0.0546875
Outputs:
- activation: bfloat16 [1024, 49152], P('col', 'row')
- weight_grad: bfloat16 [12288, 49152], P('col', 'row')
Inputs may be any that keep to these rules, and one draw needn't show every extreme that they name: The sampled blocks are the first active_blocks[0] blocks of 3072 hidden units.
All inputs are finite; a program needn't handle non-finite values.
Results may differ from a plain program's by a relative error of at most 0.001.
Values may be sent and summed in bfloat16 or wider, within the bound.
A program may use at most 640 MiB of HBM per device.

v0:
```python
import jax
import jax.numpy as jnp
from jax import lax
from jax.sharding import PartitionSpec as P

BLOCK = 3072


def in_one_piece(arrays, axis, dim, along):
    both = jnp.concatenate(arrays, axis=along)
    result, at, outs = (lax.all_gather(both, axis, axis=dim, tiled=True), 0, [])
    for a in arrays:
        outs.append(lax.slice_in_dim(result, at, at + a.shape[along], axis=along))
        at += a.shape[along]
    return tuple(outs)


def shards(tokens, prev_tokens, hidden_grad, active_blocks, weight):
    local_units = weight.shape[1]
    first_unit = lax.axis_index("row") * local_units
    unit_limit = active_blocks[0] * BLOCK
    unit_ids = first_unit + lax.iota(jnp.int32, local_units)
    unit_mask = (unit_ids < unit_limit).astype(jnp.float32)
    gathered, earlier = in_one_piece((tokens, prev_tokens), "row", 0, 1)
    hidden = lax.psum_scatter(
        jnp.dot(gathered, weight, preferred_element_type=jnp.float32),
        "col",
        scatter_dimension=0,
        tiled=True,
    )
    activation = (jax.nn.gelu(hidden, approximate=False) * unit_mask).astype(jnp.bfloat16)
    grad_sum = lax.dot_general(
        earlier,
        lax.all_gather(hidden_grad, "col", axis=0, tiled=True),
        (((0,), (0,)), ((), ())),
        preferred_element_type=jnp.float32,
    )
    weight_grad = (grad_sum * unit_mask).astype(jnp.bfloat16)
    return (activation, weight_grad)


def solution(mesh):
    return jax.shard_map(
        shards,
        mesh=mesh,
        in_specs=(P("row", "col"), P("row", "col"), P("col", "row"), P(), P("col", "row")),
        out_specs=(P("col", "row"), P("col", "row")),
        check_vma=False,
    )
```

profile of v0, /device:TPU:1, one launch (start us, length us, event | category | flops | bytes accessed | tf_op | source)
XLA Modules:
  0.0 302.3 jit_solution(265817429871638443)
XLA Ops:
  7.2 0.0 all-gather.3.cloned.1.call-start
  7.2 1.8 pad_maximum_fusion
  9.0 0.0 all-gather.3.cloned.1.call-update
  9.0 0.0 all-gather.5.cloned.1.call-start
  9.1 0.7 all-gather.5.cloned.1.call-update
  9.8 0.0 reduce-scatter.2.cloned.1.call-start
  9.8 65.9 %all-gather.3.cloned.1.call-done = bf16[1024,1536]{1,0:T(8,128)(2,1)} async-done(((bf16[128,1536]{1,0:T(8,128)(2,1)}), bf16[1024,1536]{1,0:T(8,128)(2,1)}) %all-gather.3.cloned.1.call-update) | async-done | bytes 3145744 | tf_op jit(solution)/shard_map/all_gather | solution.py:11
  75.8 17.5 %fusion.5 = f32[1024,6144]{1,0:T(8,128)} fusion(bf16[768,6144]{1,0:T(8,128)(2,1)} %param.9, bf16[1024,1536]{1,0:T(8,128)(2,1)} %all-gather.3.cloned.1.call-done), kind=kOutput, calls=%fused_computation.7 | convolution fusion | flops 9663676416 | bytes 36175872 | tf_op jit(solution)/shard_map/dot_general | solution.py:26
  93.3 0.0 copy-start
  93.3 0.0 reduce-scatter.2.cloned.1.call-update
  94.2 54.0 %all-gather.5.cloned.1.call-done = bf16[1024,6144]{1,0:T(8,128)(2,1)} async-done(((bf16[64,6144]{1,0:T(8,128)(2,1)}), bf16[1024,6144]{1,0:T(8,128)(2,1)}) %all-gather.5.cloned.1.call-update) | async-done | bytes 12582928 | tf_op jit(solution)/shard_map/all_gather | solution.py:34
  148.2 0.0 copy-done
  148.2 16.8 %multiply_convert_fusion = bf16[768,6144]{1,0:T(8,128)(2,1)} fusion(bf16[1024,6144]{1,0:T(8,128)(2,1)} %all-gather.5.cloned.1.call-done, f32[6144]{0:T(1024)S(1)} %fusion.14, bf16[1024,1536]{1,0:T(8,128)(2,1)S(1)} %copy-done), kind=kOutput, calls=%fused_computation | convolution fusion | flops 9673113600 | bytes 23617536 | tf_op jit(solution)/shard_map/dot_general | solution.py:32
  164.9 125.5 %reduce-scatter.2.cloned.1.call-done = f32[64,6144]{1,0:T(8,128)} async-done(((f32[1024,6144]{1,0:T(8,128)}), f32[64,6144]{1,0:T(8,128)}) %reduce-scatter.2.cloned.1.call-update) | async-done | bytes 1572880 | tf_op jit(solution)/shard_map/reduce_scatter | solution.py:25
  290.4 5.3 %fusion.3 = bf16[64,6144]{1,0:T(8,128)(2,1)} fusion(f32[64,6144]{1,0:T(8,128)} %reduce-scatter.2.cloned.1.call-done, f32[6144]{0:T(1024)S(1)} %fusion.14), kind=kLoop, calls=%fused_computation.5 | loop fusion | flops 25952256 | bytes 2383872 | tf_op jit(solution)/shard_map/convert_element_type | solution.py:31
  (1 shorter events, 0.0 us)
Async XLA Ops:
  7.2 68.6 %all-gather.3.cloned.1.call-start = ((), (), s32[]{:S(2)}) async-start(), calls=%async_computation.1 | async-start | bytes 3538944 | tf_op jit(solution)/shard_map/all_gather | solution.py:11
  9.0 139.1 %all-gather.5.cloned.1.call-start = ((), (), s32[]{:S(2)}) async-start(), calls=%async_computation.3 | async-start | bytes 13369344 | tf_op jit(solution)/shard_map/all_gather | solution.py:34
  9.8 280.7 %reduce-scatter.2.cloned.1.call-start = ((), (), s32[]{:S(2)}) async-start(), calls=%async_computation.2 | async-start | bytes 26738688 | tf_op jit(solution)/shard_map/reduce_scatter | solution.py:25
  93.3 54.9 %copy-start = (bf16[1024,1536]{1,0:T(8,128)(2,1)S(1)}, bf16[1024,1536]{1,0:T(8,128)(2,1)}, u32[]{:S(2)}) copy-start(bf16[1024,1536]{1,0:T(8,128)(2,1)} %all-gather.3.cloned.1.call-done) | copy-start | bytes 9437188
Sparse Core Ops, SparseCore 0:
  10.8 64.8 all-gather.2
  77.5 70.6 all-gather.4
  150.6 139.8 reduce-scatter.1
where the time goes:
time: 303 us; the launch traced here: 302 us
  waiting for transfers between devices  246 us (81%)
  matrix products  34.3 us (11%)
  between operations  14.6 us (5%)
  other arithmetic  7.08 us (2%)
    reduce_scatter x1, waiting for transfers between devices, shards(): lax.psum_scatter(jnp.dot(gathered, weight, preferred_element_type=jnp.flo...  126 us
    all_gather x1, waiting for transfers between devices, in_one_piece(): result, at, outs = (lax.all_gather(both, axis, axis=dim, tiled=True), 0, [])  65.9 us
    all_gather x1, waiting for transfers between devices, shards(): lax.all_gather(hidden_grad, 'col', axis=0, tiled=True)  54 us
    dot_general x1, matrix products, shards(): jnp.dot(gathered, weight, preferred_element_type=jnp.float32)  17.5 us
    dot_general x1, matrix products, shards(): lax.dot_general(earlier, lax.all_gather(hidden_grad, 'col', axis=0, tiled...  16.8 us
  transfers between devices with their start and end apart: 3, of which 3 were waited for; matrix products, arithmetic and copies ran while one was open for 11% of the time, Pallas kernels for 0%

commit v1 on v0

v1 whole, which is shorter than its diff:
```python
import jax
import jax.numpy as jnp
from jax import lax
from jax.experimental import pallas as pl
from jax.experimental.pallas import tpu as pltpu
from jax.sharding import PartitionSpec as P

BLOCK = 3072
MESH = pl.DeviceIdType.MESH
TB = 128
A_COLS = 1024
A_PIECES = ((0, 512), (512, 512))
B_PIECES = ((1024, 1024), (2048, 1024))
GA = 3584
GSTEP = 512
N_COPIES = 96


def kernel(tok, prev, hg, w, hid, g, xs, pv, pvt, ws, gs, part, gst,
           ax_s, ax_r, ay_s, ay_r, by_s, by_r, bx_s, bx_r,
           axs_s, axs_r, ays_s, ays_r, bys_s, bys_r, bxs_s, bxs_r,
           ssem, rsem, lsem, gsem):
    row, col = lax.axis_index("row"), lax.axis_index("col")
    z, c = lax.rem(row, 4), lax.rem(col, 2)
    half = lax.div(col, 2)
    y, xl = lax.rem(half, 4), lax.div(half, 4)
    zb, yb = row - z, xl * 8 + c
    yp, ym, y2 = lax.rem(y + 1, 4), lax.rem(y + 3, 4), lax.rem(y + 2, 4)
    zp, zm, z2 = lax.rem(z + 1, 4), lax.rem(z + 3, 4), lax.rem(z + 2, 4)
    xo = 1 - xl
    rowx = lax.rem(row + 4, 8)
    zbx = rowx - z
    d_cp = (row, col + 1 - 2 * c)
    d_xp = (row, lax.rem(col + 8, 16))
    d_yp, d_ym = (row, yb + yp * 2), (row, yb + ym * 2)
    d_hx = (rowx, col)
    d_zp, d_zm = (zb + zp, col), (zb + zm, col)

    barrier = pltpu.get_barrier_semaphore()
    peers = (d_cp, d_xp, d_yp, d_ym, d_hx, d_zp, d_zm)
    for d in peers:
        pl.semaphore_signal(barrier, inc=1, device_id=d, device_id_type=MESH)
    pl.semaphore_wait(barrier, len(peers))

    sent = []

    def send(src, dst, dev):
        k = len(sent)
        copy = pltpu.make_async_remote_copy(
            src_ref=src, dst_ref=dst, send_sem=ssem.at[k], recv_sem=rsem.at[k],
            device_id=dev, device_id_type=MESH)
        copy.start()
        sent.append(copy)
        return copy

    def local(k, src, dst):
        copy = pltpu.make_async_copy(src, dst, lsem.at[k])
        copy.start()
        return copy

    def got(*copies):
        for copy in copies:
            copy.wait_recv()

    slab = pl.ds(pl.multiple_of(c * 768, 128), 768)
    mine = pl.ds(pl.multiple_of(c * 3072, 128), 3072)
    other = pl.ds(pl.multiple_of((1 - c) * 3072, 128), 3072)
    ca, cb = pl.ds(0, GA), pl.ds(GA, 6144 - GA)
    hb = (6144 - GA) // 2
    cb0, cb1 = pl.ds(GA, hb), pl.ds(GA + hb, hb)

    def xrow(r):
        return xs.at[r, :, slab]

    def grow(xx, yy, cols):
        return gs.at[xx * 4 + yy, c, :, cols]

    t_x = send(tok, xrow(row), d_hx)
    t_op = send(tok, xrow(row), d_zp)
    t_om = send(tok, xrow(row), d_zm)
    h_x = send(hg.at[:, ca], grow(xl, y, ca), d_xp)
    h_op = send(hg.at[:, ca], grow(xl, y, ca), d_yp)
    h_om = send(hg.at[:, ca], grow(xl, y, ca), d_ym)
    w_c = send(w.at[:, other], ws.at[slab, :], d_cp)
    t_c = [send(tok, xrow(row), d_cp)]
    b_op = send(hg.at[:, cb], grow(xl, y, cb), d_yp)
    b_om = send(hg.at[:, cb], grow(xl, y, cb), d_ym)
    b_x = [send(hg.at[:, cb], grow(xl, y, cb), d_xp)]
    l_t = local(0, tok, xrow(row))
    l_w = local(1, w.at[:, mine], ws.at[slab, :])
    l_h = local(2, hg, gs.at[xl * 4 + y, c])
    l_p = local(3, prev, pv.at[row])

    got(t_x)
    t_pp = send(xrow(rowx), xrow(rowx), d_zp)
    t_pm = send(xrow(rowx), xrow(rowx), d_zm)
    t_c.append(send(xrow(rowx), xrow(rowx), d_cp))
    p_x = send(prev, pv.at[row], d_hx)
    got(h_x)
    h_pp = send(grow(xo, y, ca), grow(xo, y, ca), d_yp)
    h_pm = send(grow(xo, y, ca), grow(xo, y, ca), d_ym)
    got(t_op, t_om)
    t_f0 = send(xrow(zb + zm), xrow(zb + zm), d_zp)
    t_c.append(send(xrow(zb + zm), xrow(zb + zm), d_cp))
    t_c.append(send(xrow(zb + zp), xrow(zb + zp), d_cp))
    got(h_op, h_om)
    h_f0 = send(grow(xl, ym, ca), grow(xl, ym, ca), d_yp)
    got(t_pp, t_pm)
    t_f1 = send(xrow(zbx + zp), xrow(zbx + zp), d_zm)
    t_c.append(send(xrow(zbx + zm), xrow(zbx + zm), d_cp))
    t_c.append(send(xrow(zbx + zp), xrow(zbx + zp), d_cp))
    p_op = send(prev, pv.at[row], d_zp)
    p_om = send(prev, pv.at[row], d_zm)
    got(b_op, b_om)
    b_f0 = send(grow(xl, ym, cb0), grow(xl, ym, cb0), d_yp)
    b_f1 = send(grow(xl, yp, cb1), grow(xl, yp, cb1), d_ym)
    b_x.append(send(grow(xl, ym, cb), grow(xl, ym, cb), d_xp))
    b_x.append(send(grow(xl, yp, cb), grow(xl, yp, cb), d_xp))
    got(t_f0, t_f1)
    t_c.append(send(xrow(zb + z2), xrow(zb + z2), d_cp))
    t_c.append(send(xrow(zbx + z2), xrow(zbx + z2), d_cp))
    l_t.wait()
    l_w.wait()
    got(w_c, *t_c)

    def product(lo, hi):
        def tile(i, carry):
            cols = pl.ds(pl.multiple_of(i * 256, 256), 256)
            part[:, cols] = jnp.dot(
                xs[...].reshape(1024, 1536), ws[:, cols], preferred_element_type=jnp.float32)
            return carry

        lax.fori_loop(lo // 256, hi // 256, tile, 0)

    def prow(xx, yy):
        return pl.ds(pl.multiple_of((xx * 4 + yy) * TB, TB), TB)

    def quant(rows, c0, n, q, s):
        def peak(k, m):
            v = part[rows, pl.ds(pl.multiple_of(c0 + k * 128, 128), 128)]
            return jnp.maximum(m, jnp.max(jnp.abs(v.reshape(16, 8, 128)), axis=0))

        m = lax.fori_loop(0, n // 128, peak, jnp.full((8, 128), 1e-30, jnp.float32))
        s[...] = m * (1.0 / 32766.0)
        inv = 32766.0 / m

        def code(k, carry):
            v = part[rows, pl.ds(pl.multiple_of(c0 + k * 128, 128), 128)]
            v = (v.reshape(16, 8, 128) * inv[None]).reshape(TB, 128)
            q[:, pl.ds(pl.multiple_of(k * 128, 128), 128)] = (
                jnp.round(v).astype(jnp.int32).astype(jnp.int16))
            return carry

        lax.fori_loop(0, n // 128, code, 0)

    def add(rows, c0, n, q, s):
        def step(k, carry):
            cols = pl.ds(pl.multiple_of(c0 + k * 128, 128), 128)
            v = q[:, pl.ds(pl.multiple_of(k * 128, 128), 128)].astype(jnp.int32).astype(jnp.float32)
            v = (v.reshape(16, 8, 128) * s[...][None]).reshape(TB, 128)
            part[rows, cols] = part[rows, cols] + v
            return carry

        lax.fori_loop(0, n // 128, step, 0)

    def send2(qs, ss, qr, sr, dev):
        return send(ss, sr, dev), send(qs, qr, dev)

    def a_first(i):
        c0, n = A_PIECES[i]
        for yy in range(4):
            quant(prow(xo, yy), c0, n, ax_s.at[i, yy], axs_s.at[i, yy])
        return send2(ax_s.at[i], axs_s.at[i], ax_r.at[i], axs_r.at[i], d_xp)

    def a_second(i, first):
        c0, n = A_PIECES[i]
        yd, yo, d_d, d_o = (yp, ym, d_yp, d_ym) if i % 2 == 0 else (ym, yp, d_ym, d_yp)
        got(*first)
        for yy in range(4):
            add(prow(xl, yy), c0, n, ax_r.at[i, yy], axs_r.at[i, yy])
        far = by_y(ay_s, ay_r, ays_s, ays_r, i, 0, prow(xl, y2), c0, n, d_d)
        near = by_y(ay_s, ay_r, ays_s, ays_r, i, 1, prow(xl, yo), c0, n, d_o)
        return far, near

    def by_y(qs, qr, ss, sr, i, k, rows, c0, n, dev):
        quant(rows, c0, n, qs.at[i, k], ss.at[i, k])
        return send2(qs.at[i, k], ss.at[i, k], qr.at[i, k], sr.at[i, k], dev)

    def a_third(i, far):
        c0, n = A_PIECES[i]
        yd, d_d = (yp, d_yp) if i % 2 == 0 else (ym, d_ym)
        got(*far)
        add(prow(xl, yd), c0, n, ay_r.at[i, 0], ays_r.at[i, 0])
        return by_y(ay_s, ay_r, ays_s, ays_r, i, 2, prow(xl, yd), c0, n, d_d)

    def a_last(i, near, passed):
        c0, n = A_PIECES[i]
        got(*near, *passed)
        add(prow(xl, y), c0, n, ay_r.at[i, 1], ays_r.at[i, 1])
        add(prow(xl, y), c0, n, ay_r.at[i, 2], ays_r.at[i, 2])

    def b_y(i, k, rows, dev):
        c0, n = B_PIECES[i]
        return by_y(by_s, by_r, bys_s, bys_r, i, k, rows, c0, n, dev)

    def b_first(i):
        return (b_y(i, 0, prow(0, y2), d_yp), b_y(i, 1, prow(1, y2), d_ym),
                b_y(i, 2, prow(1, yp), d_yp), b_y(i, 3, prow(0, ym), d_ym))

    def b_second(i, first):
        c0, n = B_PIECES[i]
        got(*first[0])
        add(prow(0, yp), c0, n, by_r.at[i, 0], bys_r.at[i, 0])
        up = b_y(i, 4, prow(0, yp), d_yp)
        got(*first[1])
        add(prow(1, ym), c0, n, by_r.at[i, 1], bys_r.at[i, 1])
        down = b_y(i, 5, prow(1, ym), d_ym)
        return up, down

    def b_third(i, first, second):
        c0, n = B_PIECES[i]
        got(*first[2], *first[3])
        add(prow(1, y), c0, n, by_r.at[i, 2], bys_r.at[i, 2])
        add(prow(0, y), c0, n, by_r.at[i, 3], bys_r.at[i, 3])
        got(*second[0], *second[1])
        add(prow(0, y), c0, n, by_r.at[i, 4], bys_r.at[i, 4])
        add(prow(1, y), c0, n, by_r.at[i, 5], bys_r.at[i, 5])
        quant(prow(xo, y), c0, n, bx_s.at[i], bxs_s.at[i])
        return send2(bx_s.at[i], bxs_s.at[i], bx_r.at[i], bxs_r.at[i], d_xp)

    def b_last(i, third):
        c0, n = B_PIECES[i]
        got(*third)
        add(prow(xl, y), c0, n, bx_r.at[i], bxs_r.at[i])

    def grad(lo, hi):
        def tile(i, carry):
            cols = pl.ds(pl.multiple_of(i * GSTEP, GSTEP), GSTEP)
            slot = lax.rem(i, 2)

            @pl.when(i >= 2)
            def _():
                pltpu.make_async_copy(gst.at[slot], g.at[:, cols], gsem.at[slot]).wait()

            gst[slot] = jnp.dot(
                pvt[...], gs[:, :, :, cols].reshape(1024, GSTEP),
                preferred_element_type=jnp.float32).astype(jnp.bfloat16)
            pltpu.make_async_copy(gst.at[slot], g.at[:, cols], gsem.at[slot]).start()
            return carry

        lax.fori_loop(lo, hi, tile, 0)

    product(0, A_COLS)
    a1 = [a_first(0), a_first(1)]
    got(h_pp, h_pm)
    h_f1 = send(grow(xo, yp, ca), grow(xo, yp, ca), d_ym)
    got(p_x)
    p_pp = send(pv.at[rowx], pv.at[rowx], d_zp)
    p_pm = send(pv.at[rowx], pv.at[rowx], d_zm)
    product(B_PIECES[0][0], B_PIECES[0][0] + B_PIECES[0][1])
    b1 = [b_first(0)]
    got(b_f0, b_f1)
    b_x.append(send(grow(xl, y2, cb), grow(xl, y2, cb), d_xp))
    got(p_op, p_om)
    p_f0 = send(pv.at[zb + zm], pv.at[zb + zm], d_zp)
    product(B_PIECES[1][0], B_PIECES[1][0] + B_PIECES[1][1])
    b1.append(b_first(1))
    got(p_pp, p_pm)
    p_f1 = send(pv.at[zbx + zp], pv.at[zbx + zp], d_zm)
    got(h_f0, h_f1)
    l_h.wait()
    c_a = send(gs.at[:, c, :, ca], gs.at[:, c, :, ca], d_cp)
    got(*b_x)
    c_b = send(gs.at[:, c, :, cb], gs.at[:, c, :, cb], d_cp)
    l_p.wait()
    got(p_f0, p_f1)
    pvt[...] = pv[...].reshape(1024, 768).T
    b2 = [b_second(0, b1[0])]
    n_grad = 6144 // GSTEP
    got(c_a, c_b)
    a2 = [a_second(0, a1[0])]
    b2.append(b_second(1, b1[1]))
    grad(0, n_grad // 3)
    a2.append(a_second(1, a1[1]))
    a3 = [a_third(0, a2[0][0])]
    b3 = [b_third(0, b1[0], b2[0])]
    grad(n_grad // 3, 2 * n_grad // 3)
    a3.append(a_third(1, a2[1][0]))
    b3.append(b_third(1, b1[1], b2[1]))
    grad(2 * n_grad // 3, n_grad)
    for i in range(2):
        b_last(i, b3[i])
    for i in range(2):
        a_last(i, a2[i][1], a3[i])

    own = pl.ds(pl.multiple_of((xl * 4 + y) * TB + c * 64, 64), 64)
    theirs = pl.ds(pl.multiple_of((xl * 4 + y) * TB + (1 - c) * 64, 64), 64)
    last = send(part.at[theirs, :], hid.at[:, mine], d_cp)
    l_o = local(4, part.at[own, :], hid.at[:, mine])
    for slot in range(2):
        pltpu.make_async_copy(gst.at[slot], g.at[:, pl.ds(0, GSTEP)], gsem.at[slot]).wait()
    l_o.wait()
    got(last)
    for copy in sent:
        copy.wait_send()


def exchange(tokens, prev_tokens, hidden_grad, weight):
    bf, f32, i16 = jnp.bfloat16, jnp.float32, jnp.int16
    any_space = pl.BlockSpec(memory_space=pl.ANY)
    na, nb = A_PIECES[0][1], B_PIECES[0][1]

    def pair(shape, dtype):
        return [pltpu.VMEM(shape, dtype)] * 2

    return pl.pallas_call(
        kernel,
        out_shape=(
            jax.ShapeDtypeStruct((64, 6144), f32),
            jax.ShapeDtypeStruct((768, 6144), bf),
        ),
        in_specs=[any_space] * 4,
        out_specs=(any_space, any_space),
        scratch_shapes=[
            pltpu.VMEM((8, 128, 1536), bf),
            pltpu.VMEM((8, 128, 768), bf),
            pltpu.VMEM((768, 1024), bf),
            pltpu.VMEM((1536, 3072), bf),
            pltpu.VMEM((8, 2, 64, 6144), bf),
            pltpu.VMEM((1024, 3072), f32),
            pltpu.VMEM((2, 768, GSTEP), bf),
            *pair((2, 4, TB, na), i16),
            *pair((2, 3, TB, na), i16),
            *pair((2, 6, TB, nb), i16),
            *pair((2, TB, nb), i16),
            *pair((2, 4, 8, 128), f32),
            *pair((2, 3, 8, 128), f32),
            *pair((2, 6, 8, 128), f32),
            *pair((2, 8, 128), f32),
            pltpu.SemaphoreType.DMA((N_COPIES,)),
            pltpu.SemaphoreType.DMA((N_COPIES,)),
            pltpu.SemaphoreType.DMA((5,)),
            pltpu.SemaphoreType.DMA((2,)),
        ],
        compiler_params=pltpu.CompilerParams(
            collective_id=0, has_side_effects=True, vmem_limit_bytes=67043328),
    )(tokens, prev_tokens, hidden_grad, weight)


def shards(tokens, prev_tokens, hidden_grad, active_blocks, weight):
    local_units = weight.shape[1]
    first_unit = lax.axis_index("row") * local_units
    unit_ids = first_unit + lax.iota(jnp.int32, local_units)
    active = unit_ids < active_blocks[0] * BLOCK
    hidden, grad = exchange(tokens, prev_tokens, hidden_grad, weight)
    activation = jnp.where(active, jax.nn.gelu(hidden, approximate=False), 0.0).astype(jnp.bfloat16)
    weight_grad = jnp.where(active, grad, jnp.zeros((), jnp.bfloat16))
    return (activation, weight_grad)


def solution(mesh):
    return jax.shard_map(
        shards,
        mesh=mesh,
        in_specs=(P("row", "col"), P("row", "col"), P("col", "row"), P(), P("col", "row")),
        out_specs=(P("col", "row"), P("col", "row")),
        check_vma=False,
    )
```

time: 303 us -> 125 us (0.41)
  waiting for transfers between devices: 246 us -> 0 us
  Pallas kernels: 0 us -> 109 us
  matrix products: 34.3 us -> 0 us
  between operations: 14.6 us -> 1.3 us
  other arithmetic: 7.08 us -> 14 us
    reduce_scatter x1 -> x0, waiting for transfers between devices: 126 us -> none  [shards(): lax.psum_scatter(jnp.dot(gathered, weight, preferred_element_type=jnp.flo...]
    all_gather x2 -> x0, waiting for transfers between devices: 120 us -> none  [the longest x1 65.9 us: in_one_piece(): result, at, outs = (lax.all_gather(both, axis, axis=dim, tiled=True), 0, [])]
    pallas_call x0 -> x1, Pallas kernels: none -> 109 us  [exchange(): pl.pallas_call(kernel, out_shape=(jax.ShapeDtypeStruct((64, 6144), f32),...]
    dot_general x2 -> x0, matrix products: 34.3 us -> none  [the longest x1 17.5 us: shards(): jnp.dot(gathered, weight, preferred_element_type=jnp.float32)]
    select_n x0 -> x1, other arithmetic: none -> 8.12 us  [shards(): weight_grad = jnp.where(active, grad, jnp.zeros((), jnp.bfloat16))]
  transfers between devices with their start and end apart: 3 -> 0, of which waited for: 3 -> 0; matrix products, arithmetic and copies ran while one was open for 11% -> 0% of each run, Pallas kernels for 0% -> 0%
where the time goes in v1:
time: 125 us; the launch traced here: 124 us
  Pallas kernels  109 us (87%)
  other arithmetic  14 us (11%)
  between operations  1.3 us (1%)
    pallas_call x1, Pallas kernels, exchange(): pl.pallas_call(kernel, out_shape=(jax.ShapeDtypeStruct((64, 6144), f32),...  109 us
    select_n x1, other arithmetic, shards(): weight_grad = jnp.where(active, grad, jnp.zeros((), jnp.bfloat16))  8.12 us
    convert_element_type x1, other arithmetic, shards(): jnp.where(active, jax.nn.gelu(hidden, approximate=False), 0.0)  5.31 us

profile of v1, /device:TPU:1, one launch (start us, length us, event | category | flops | bytes accessed | tf_op | source)
XLA Modules:
  0.0 124.4 jit_solution(3723164207030793149)
XLA Ops:
  1.3 0.6 add_compare_fusion
  1.9 109.1 %shard_map.68 = (f32[64,6144]{1,0:T(8,128)}, bf16[768,6144]{1,0:T(8,128)(2,1)}) custom-call(bf16[128,768]{1,0:T(8,128)(2,1)} %tok.1, bf16[128,768]{1,0:T(8,128)(2,1)} %prev.1, bf16[64,6144]{1,0:T(8,128)(2,1)} %hg.1, bf16[768,6144]{1,0:T(8,128)(2,1)} %w.1), custom_call_target="tpu_custom_call" | custom-call | tf_op jit(solution)/shard_map/pallas_call | solution.py:316
  111.0 0.0 copy-start
  111.0 5.3 %fusion.3 = bf16[64,6144]{1,0:T(8,128)(2,1)} fusion(f32[64,6144]{1,0:T(8,128)} %get-tuple-element.4, pred[6144]{0:T(1024)(128)(4,1)} %add_compare_fusion), kind=kLoop, calls=%fused_computation.5 | loop fusion | flops 25952256 | bytes 2365440 | tf_op jit(solution)/shard_map/convert_element_type | solution.py:356
  116.3 0.0 copy-done
  116.3 8.1 %broadcast_select_fusion = bf16[768,6144]{1,0:T(8,128)(2,1)} fusion(bf16[768,6144]{1,0:T(8,128)(2,1)} %get-tuple-element.5, pred[6144]{0:T(1024)(128)(4,1)S(1)} %copy-done), kind=kLoop, calls=%fused_computation | loop fusion | flops 4718592 | bytes 18880512 | tf_op jit(solution)/shard_map/jit(_where)/select_n | solution.py:357
Async XLA Ops:
  111.0 5.3 %copy-start = (pred[6144]{0:T(1024)(128)(4,1)S(1)}, pred[6144]{0:T(1024)(128)(4,1)}, u32[]{:S(2)}) copy-start(pred[6144]{0:T(1024)(128)(4,1)} %add_compare_fusion) | copy-start | bytes 18436

commit v2 on v1

--- a/solution.py
+++ b/solution.py
@@ -10,16 +10,17 @@
 TB = 128
 A_COLS = 1024
 A_PIECES = ((0, 512), (512, 512))
-B_PIECES = ((1024, 1024), (2048, 1024))
+B_PIECES = ((1024, 512), (1536, 512), (2048, 512), (2560, 512))
 GA = 3584
 GSTEP = 512
-N_COPIES = 96
-
-
-def kernel(tok, prev, hg, w, hid, g, xs, pv, pvt, ws, gs, part, gst,
+N_COPIES = 136
+VMEM_LIMIT = 54 * 1000 * 1000
+
+
+def kernel(active, tok, prev, hg, w, act, g, xs, pv, pvt, gs, part, actv,
            ax_s, ax_r, ay_s, ay_r, by_s, by_r, bx_s, bx_r,
            axs_s, axs_r, ays_s, ays_r, bys_s, bys_r, bxs_s, bxs_r,
-           ssem, rsem, lsem, gsem):
+           ssem, rsem, lsem):
     row, col = lax.axis_index("row"), lax.axis_index("col")
     z, c = lax.rem(row, 4), lax.rem(col, 2)
     half = lax.div(col, 2)
@@ -81,13 +82,13 @@
     h_x = send(hg.at[:, ca], grow(xl, y, ca), d_xp)
     h_op = send(hg.at[:, ca], grow(xl, y, ca), d_yp)
     h_om = send(hg.at[:, ca], grow(xl, y, ca), d_ym)
-    w_c = send(w.at[:, other], ws.at[slab, :], d_cp)
+    w_c = send(w.at[:, other], g.at[:, mine], d_cp)
     t_c = [send(tok, xrow(row), d_cp)]
     b_op = send(hg.at[:, cb], grow(xl, y, cb), d_yp)
     b_om = send(hg.at[:, cb], grow(xl, y, cb), d_ym)
     b_x = [send(hg.at[:, cb], grow(xl, y, cb), d_xp)]
     l_t = local(0, tok, xrow(row))
-    l_w = local(1, w.at[:, mine], ws.at[slab, :])
+    l_w = local(1, w.at[:, mine], g.at[:, mine])
     l_h = local(2, hg, gs.at[xl * 4 + y, c])
     l_p = local(3, prev, pv.at[row])
 
@@ -96,24 +97,24 @@
     t_pm = send(xrow(rowx), xrow(rowx), d_zm)
     t_c.append(send(xrow(rowx), xrow(rowx), d_cp))
     p_x = send(prev, pv.at[row], d_hx)
-    got(h_x)
-    h_pp = send(grow(xo, y, ca), grow(xo, y, ca), d_yp)
-    h_pm = send(grow(xo, y, ca), grow(xo, y, ca), d_ym)
     got(t_op, t_om)
     t_f0 = send(xrow(zb + zm), xrow(zb + zm), d_zp)
     t_c.append(send(xrow(zb + zm), xrow(zb + zm), d_cp))
     t_c.append(send(xrow(zb + zp), xrow(zb + zp), d_cp))
-    got(h_op, h_om)
-    h_f0 = send(grow(xl, ym, ca), grow(xl, ym, ca), d_yp)
     got(t_pp, t_pm)
     t_f1 = send(xrow(zbx + zp), xrow(zbx + zp), d_zm)
     t_c.append(send(xrow(zbx + zm), xrow(zbx + zm), d_cp))
     t_c.append(send(xrow(zbx + zp), xrow(zbx + zp), d_cp))
     p_op = send(prev, pv.at[row], d_zp)
     p_om = send(prev, pv.at[row], d_zm)
+    got(h_x)
+    h_pp = send(grow(xo, y, ca), grow(xo, y, ca), d_yp)
+    h_pm = send(grow(xo, y, ca), grow(xo, y, ca), d_ym)
+    got(h_op, h_om)
+    h_f0 = send(grow(xl, ym, ca), grow(xl, ym, ca), d_yp)
     got(b_op, b_om)
+    b_f1 = send(grow(xl, yp, cb1), grow(xl, yp, cb1), d_ym)
     b_f0 = send(grow(xl, ym, cb0), grow(xl, ym, cb0), d_yp)
-    b_f1 = send(grow(xl, yp, cb1), grow(xl, yp, cb1), d_ym)
     b_x.append(send(grow(xl, ym, cb), grow(xl, ym, cb), d_xp))
     b_x.append(send(grow(xl, yp, cb), grow(xl, yp, cb), d_xp))
     got(t_f0, t_f1)
@@ -126,8 +127,11 @@
     def product(lo, hi):
         def tile(i, carry):
             cols = pl.ds(pl.multiple_of(i * 256, 256), 256)
+            cols2 = pl.ds(pl.multiple_of(i * 256 + 3072, 256), 256)
             part[:, cols] = jnp.dot(
-                xs[...].reshape(1024, 1536), ws[:, cols], preferred_element_type=jnp.float32)
+                xs[...].reshape(1024, 1536),
+                jnp.concatenate([g[:, cols], g[:, cols2]], axis=0),
+                preferred_element_type=jnp.float32)
             return carry
 
         lax.fori_loop(lo // 256, hi // 256, tile, 0)
@@ -198,14 +202,17 @@
         got(*near, *passed)
         add(prow(xl, y), c0, n, ay_r.at[i, 1], ays_r.at[i, 1])
         add(prow(xl, y), c0, n, ay_r.at[i, 2], ays_r.at[i, 2])
+        finish(c0, n)
 
     def b_y(i, k, rows, dev):
         c0, n = B_PIECES[i]
         return by_y(by_s, by_r, bys_s, bys_r, i, k, rows, c0, n, dev)
 
     def b_first(i):
-        return (b_y(i, 0, prow(0, y2), d_yp), b_y(i, 1, prow(1, y2), d_ym),
-                b_y(i, 2, prow(1, yp), d_yp), b_y(i, 3, prow(0, ym), d_ym))
+        return b_y(i, 0, prow(0, y2), d_yp), b_y(i, 1, prow(1, y2), d_ym)
+
+    def b_near(i):
+        return b_y(i, 2, prow(1, yp), d_yp), b_y(i, 3, prow(0, ym), d_ym)
 
     def b_second(i, first):
         c0, n = B_PIECES[i]
@@ -217,9 +224,9 @@
         down = b_y(i, 5, prow(1, ym), d_ym)
         return up, down
 
-    def b_third(i, first, second):
+    def b_third(i, near, second):
         c0, n = B_PIECES[i]
-        got(*first[2], *first[3])
+        got(*near[0], *near[1])
         add(prow(1, y), c0, n, by_r.at[i, 2], bys_r.at[i, 2])
         add(prow(0, y), c0, n, by_r.at[i, 3], bys_r.at[i, 3])
         got(*second[0], *second[1])
@@ -232,130 +239,169 @@
         c0, n = B_PIECES[i]
         got(*third)
         add(prow(xl, y), c0, n, bx_r.at[i], bxs_r.at[i])
+        finish(c0, n)
+
+    unit_limit = active[0] * BLOCK - row * 6144
+
+    def unit_mask(first, rows, n):
+        return first + lax.broadcasted_iota(jnp.int32, (rows, n), 1) < unit_limit
 
     def grad(lo, hi):
         def tile(i, carry):
             cols = pl.ds(pl.multiple_of(i * GSTEP, GSTEP), GSTEP)
-            slot = lax.rem(i, 2)
-
-            @pl.when(i >= 2)
-            def _():
-                pltpu.make_async_copy(gst.at[slot], g.at[:, cols], gsem.at[slot]).wait()
-
-            gst[slot] = jnp.dot(
-                pvt[...], gs[:, :, :, cols].reshape(1024, GSTEP),
-                preferred_element_type=jnp.float32).astype(jnp.bfloat16)
-            pltpu.make_async_copy(gst.at[slot], g.at[:, cols], gsem.at[slot]).start()
+            v = jnp.dot(pvt[...], gs[:, :, :, cols].reshape(1024, GSTEP),
+                        preferred_element_type=jnp.float32)
+            g[:, cols] = jnp.where(unit_mask(i * GSTEP, 768, GSTEP), v, 0.0).astype(jnp.bfloat16)
             return carry
 
         lax.fori_loop(lo, hi, tile, 0)
 
+    own_rows = pl.ds(pl.multiple_of(c * 64, 64), 64)
+    their_rows = pl.ds(pl.multiple_of((1 - c) * 64, 64), 64)
+    finals = []
+
+    def finish(c0, n):
+        def step(k, carry):
+            at = pl.multiple_of(c0 + k * 128, 128)
+            v = part[prow(xl, y), pl.ds(at, 128)]
+            v = v * (lax.erf(v * 0.7071067811865476) + 1.0) * 0.5
+            v = jnp.where(unit_mask(c * 3072 + at, TB, 128), v, 0.0)
+            actv[:, pl.ds(at, 128)] = v.astype(jnp.bfloat16)
+            return carry
+
+        lax.fori_loop(0, n // 128, step, 0)
+        cols = pl.ds(pl.multiple_of(c * 3072 + c0, 128), n)
+        finals.append(send(actv.at[their_rows, pl.ds(c0, n)], act.at[:, cols], d_cp))
+        act[:, cols] = actv[own_rows, pl.ds(c0, n)]
+
     product(0, A_COLS)
-    a1 = [a_first(0), a_first(1)]
+    a1 = [a_first(i) for i in range(len(A_PIECES))]
+    product(B_PIECES[0][0], B_PIECES[2][0])
+    b1 = [b_first(0), b_first(1)]
     got(h_pp, h_pm)
     h_f1 = send(grow(xo, yp, ca), grow(xo, yp, ca), d_ym)
     got(p_x)
     p_pp = send(pv.at[rowx], pv.at[rowx], d_zp)
     p_pm = send(pv.at[rowx], pv.at[rowx], d_zm)
-    product(B_PIECES[0][0], B_PIECES[0][0] + B_PIECES[0][1])
-    b1 = [b_first(0)]
-    got(b_f0, b_f1)
-    b_x.append(send(grow(xl, y2, cb), grow(xl, y2, cb), d_xp))
+    got(b_f1)
+    b_x.append(send(grow(xl, y2, cb1), grow(xl, y2, cb1), d_xp))
+    product(B_PIECES[2][0], 3072)
+    b1 += [b_first(2), b_first(3)]
     got(p_op, p_om)
     p_f0 = send(pv.at[zb + zm], pv.at[zb + zm], d_zp)
-    product(B_PIECES[1][0], B_PIECES[1][0] + B_PIECES[1][1])
-    b1.append(b_first(1))
+    b1n = [b_near(i) for i in range(4)]
     got(p_pp, p_pm)
     p_f1 = send(pv.at[zbx + zp], pv.at[zbx + zp], d_zm)
-    got(h_f0, h_f1)
+    got(h_f0)
+    got(b_f0)
+    b_x.append(send(grow(xl, y2, cb0), grow(xl, y2, cb0), d_xp))
     l_h.wait()
+    near_rows, far_rows = pl.ds(xl * 4, 4), pl.ds(xo * 4, 4)
+    c_b0 = send(gs.at[near_rows, c, :, cb], gs.at[near_rows, c, :, cb], d_cp)
+    got(h_f1)
     c_a = send(gs.at[:, c, :, ca], gs.at[:, c, :, ca], d_cp)
-    got(*b_x)
-    c_b = send(gs.at[:, c, :, cb], gs.at[:, c, :, cb], d_cp)
+    b2 = [b_second(0, b1[0])]
     l_p.wait()
     got(p_f0, p_f1)
     pvt[...] = pv[...].reshape(1024, 768).T
-    b2 = [b_second(0, b1[0])]
-    n_grad = 6144 // GSTEP
-    got(c_a, c_b)
+    b2.append(b_second(1, b1[1]))
     a2 = [a_second(0, a1[0])]
-    b2.append(b_second(1, b1[1]))
-    grad(0, n_grad // 3)
+    got(c_a)
+    grad(0, 1)
+    b2.append(b_second(2, b1[2]))
+    grad(1, 2)
+    b2.append(b_second(3, b1[3]))
+    grad(2, 4)
     a2.append(a_second(1, a1[1]))
+    grad(4, 7)
+    b3 = [b_third(0, b1n[0], b2[0])]
+    got(*b_x)
+    c_b1 = send(gs.at[far_rows, c, :, cb], gs.at[far_rows, c, :, cb], d_cp)
+    b3.append(b_third(1, b1n[1], b2[1]))
     a3 = [a_third(0, a2[0][0])]
-    b3 = [b_third(0, b1[0], b2[0])]
-    grad(n_grad // 3, 2 * n_grad // 3)
+    got(c_b0, c_b1)
+    grad(7, 9)
+    b3.append(b_third(2, b1n[2], b2[2]))
+    grad(9, 10)
+    b3.append(b_third(3, b1n[3], b2[3]))
     a3.append(a_third(1, a2[1][0]))
-    b3.append(b_third(1, b1[1], b2[1]))
-    grad(2 * n_grad // 3, n_grad)
-    for i in range(2):
-        b_last(i, b3[i])
-    for i in range(2):
-        a_last(i, a2[i][1], a3[i])
-
-    own = pl.ds(pl.multiple_of((xl * 4 + y) * TB + c * 64, 64), 64)
-    theirs = pl.ds(pl.multiple_of((xl * 4 + y) * TB + (1 - c) * 64, 64), 64)
-    last = send(part.at[theirs, :], hid.at[:, mine], d_cp)
-    l_o = local(4, part.at[own, :], hid.at[:, mine])
-    for slot in range(2):
-        pltpu.make_async_copy(gst.at[slot], g.at[:, pl.ds(0, GSTEP)], gsem.at[slot]).wait()
-    l_o.wait()
-    got(last)
+    grad(10, 12)
+    b_last(0, b3[0])
+    b_last(1, b3[1])
+    a_last(0, a2[0][1], a3[0])
+    b_last(2, b3[2])
+    b_last(3, b3[3])
+    a_last(1, a2[1][1], a3[1])
+    got(*finals)
     for copy in sent:
         copy.wait_send()
 
 
-def exchange(tokens, prev_tokens, hidden_grad, weight):
+def exchange(active_blocks, tokens, prev_tokens, hidden_grad, weight):
     bf, f32, i16 = jnp.bfloat16, jnp.float32, jnp.int16
     any_space = pl.BlockSpec(memory_space=pl.ANY)
+    vmem = pl.BlockSpec(memory_space=pltpu.VMEM)
     na, nb = A_PIECES[0][1], B_PIECES[0][1]
+    pa, pb = len(A_PIECES), len(B_PIECES)
 
     def pair(shape, dtype):
         return [pltpu.VMEM(shape, dtype)] * 2
 
     return pl.pallas_call(
         kernel,
-        out_shape=(
-            jax.ShapeDtypeStruct((64, 6144), f32),
-            jax.ShapeDtypeStruct((768, 6144), bf),
-        ),
-        in_specs=[any_space] * 4,
-        out_specs=(any_space, any_space),
+        out_shape=(pltpu.VMEM((64, 6144), bf), pltpu.VMEM((768, 6144), bf)),
+        in_specs=[pl.BlockSpec(memory_space=pltpu.SMEM)] + [any_space] * 4,
+        out_specs=(vmem, vmem),
         scratch_shapes=[
             pltpu.VMEM((8, 128, 1536), bf),
             pltpu.VMEM((8, 128, 768), bf),
             pltpu.VMEM((768, 1024), bf),
-            pltpu.VMEM((1536, 3072), bf),
             pltpu.VMEM((8, 2, 64, 6144), bf),
             pltpu.VMEM((1024, 3072), f32),
-            pltpu.VMEM((2, 768, GSTEP), bf),
-            *pair((2, 4, TB, na), i16),
-            *pair((2, 3, TB, na), i16),
-            *pair((2, 6, TB, nb), i16),
-            *pair((2, TB, nb), i16),
-            *pair((2, 4, 8, 128), f32),
-            *pair((2, 3, 8, 128), f32),
-            *pair((2, 6, 8, 128), f32),
-            *pair((2, 8, 128), f32),
+            pltpu.VMEM((TB, 3072), bf),
+            *pair((pa, 4, TB, na), i16),
+            *pair((pa, 3, TB, na), i16),
+            *pair((pb, 6, TB, nb), i16),
+            *pair((pb, TB, nb), i16),
+            *pair((pa, 4, 8, 128), f32),
+            *pair((pa, 3, 8, 128), f32),
+            *pair((pb, 6, 8, 128), f32),
+            *pair((pb, 8, 128), f32),
             pltpu.SemaphoreType.DMA((N_COPIES,)),
             pltpu.SemaphoreType.DMA((N_COPIES,)),
-            pltpu.SemaphoreType.DMA((5,)),
-            pltpu.SemaphoreType.DMA((2,)),
+            pltpu.SemaphoreType.DMA((4,)),
         ],
         compiler_params=pltpu.CompilerParams(
-            collective_id=0, has_side_effects=True, vmem_limit_bytes=67043328),
-    )(tokens, prev_tokens, hidden_grad, weight)
+            collective_id=0, has_side_effects=True, vmem_limit_bytes=VMEM_LIMIT),
+    )(active_blocks, *(pltpu.with_memory_space_constraint(a, pltpu.HBM)
+                       for a in (tokens, prev_tokens, hidden_grad, weight)))
+
+
+def store_kernel(act, g, act_out, g_out, sems):
+    copies = [pltpu.make_async_copy(act, act_out, sems.at[4])]
+    for k in range(4):
+        rows = pl.ds(k * 192, 192)
+        copies.append(pltpu.make_async_copy(g.at[rows], g_out.at[rows], sems.at[k]))
+    for copy in copies:
+        copy.start()
+    for copy in copies:
+        copy.wait()
+
+
+def store(act, g):
+    return pl.pallas_call(
+        store_kernel,
+        out_shape=(jax.ShapeDtypeStruct(act.shape, act.dtype), jax.ShapeDtypeStruct(g.shape, g.dtype)),
+        in_specs=[pl.BlockSpec(memory_space=pltpu.VMEM)] * 2,
+        out_specs=[pl.BlockSpec(memory_space=pl.ANY)] * 2,
+        scratch_shapes=[pltpu.SemaphoreType.DMA((5,))],
+        compiler_params=pltpu.CompilerParams(vmem_limit_bytes=12 * 1024 * 1024),
+    )(act, g)
 
 
 def shards(tokens, prev_tokens, hidden_grad, active_blocks, weight):
-    local_units = weight.shape[1]
-    first_unit = lax.axis_index("row") * local_units
-    unit_ids = first_unit + lax.iota(jnp.int32, local_units)
-    active = unit_ids < active_blocks[0] * BLOCK
-    hidden, grad = exchange(tokens, prev_tokens, hidden_grad, weight)
-    activation = jnp.where(active, jax.nn.gelu(hidden, approximate=False), 0.0).astype(jnp.bfloat16)
-    weight_grad = jnp.where(active, grad, jnp.zeros((), jnp.bfloat16))
-    return (activation, weight_grad)
+    act, grad = exchange(active_blocks, tokens, prev_tokens, hidden_grad, weight)
+    return tuple(store(act, grad))
 
 
 def solution(mesh):

time: 125 us -> 102 us (0.82)
  other arithmetic: 14 us -> 0 us
  Pallas kernels: 109 us -> 101 us
    select_n x1 -> x0, other arithmetic: 8.12 us -> none  [shards(): weight_grad = jnp.where(active, grad, jnp.zeros((), jnp.bfloat16))]
    pallas_call x1 -> x2, Pallas kernels: 109 us -> 101 us  [the longest x1 97.1 us: exchange(): pl.pallas_call(kernel, out_shape=(pltpu.VMEM((64, 6144), bf), pltpu.VMEM(...]
    convert_element_type x1 -> x0, other arithmetic: 5.31 us -> none  [shards(): jnp.where(active, jax.nn.gelu(hidden, approximate=False), 0.0)]
where the time goes in v2:
time: 102 us
  Pallas kernels  101 us (99%)
  between operations  1.28 us (1%)
    pallas_call x1, Pallas kernels, exchange(): pl.pallas_call(kernel, out_shape=(pltpu.VMEM((64, 6144), bf), pltpu.VMEM(...  97.1 us
    pallas_call x1, Pallas kernels, store(): pl.pallas_call(store_kernel, out_shape=(jax.ShapeDtypeStruct(act.shape, a...  3.97 us

profile of v2, /device:TPU:1, one launch (start us, length us, event | category | flops | bytes accessed | tf_op | source)
XLA Modules:
  0.0 102.4 jit_solution(12056136271270160170)
XLA Ops:
  1.3 97.1 %shard_map.68 = (bf16[64,6144]{1,0:T(8,128)(2,1)S(1)}, bf16[768,6144]{1,0:T(8,128)(2,1)S(1)}) custom-call(s32[1]{0:T(128)S(6)} %copy.7.active, bf16[128,768]{1,0:T(8,128)(2,1)} %tok.1, bf16[128,768]{1,0:T(8,128)(2,1)} %prev.1, bf16[64,6144]{1,0:T(8,128)(2,1)} %hg.1, bf16[768,6144]{1,0:T(8,128)(2,1)} %w.1), custom_call_target="tpu_custom_call" | custom-call | tf_op jit(solution)/shard_map/pallas_call | solution.py:350
  98.4 4.0 %shard_map.69 = (bf16[64,6144]{1,0:T(8,128)(2,1)}, bf16[768,6144]{1,0:T(8,128)(2,1)}) custom-call(bf16[64,6144]{1,0:T(8,128)(2,1)S(1)} %get-tuple-element.4.act, bf16[768,6144]{1,0:T(8,128)(2,1)S(1)} %get-tuple-element.5.g), custom_call_target="tpu_custom_call" | custom-call | tf_op jit(solution)/shard_map/pallas_call | solution.py:392

commit v3 on v2

--- a/solution.py
+++ b/solution.py
@@ -13,13 +13,13 @@
 B_PIECES = ((1024, 512), (1536, 512), (2048, 512), (2560, 512))
 GA = 3584
 GSTEP = 512
-N_COPIES = 136
+N_COPIES = 95
+N_SENDS = 65
 VMEM_LIMIT = 54 * 1000 * 1000
 
 
-def kernel(active, tok, prev, hg, w, act, g, xs, pv, pvt, gs, part, actv,
-           ax_s, ax_r, ay_s, ay_r, by_s, by_r, bx_s, bx_r,
-           axs_s, axs_r, ays_s, ays_r, bys_s, bys_r, bxs_s, bxs_r,
+def kernel(active, tok, prev, hg, w, act, g, xs, pv, pvt, gs, part, oth,
+           ax_s, ax_r, ay_s, ay_r, by_s, by_r, bx_s, af_r, bf_r,
            ssem, rsem, lsem):
     row, col = lax.axis_index("row"), lax.axis_index("col")
     z, c = lax.rem(row, 4), lax.rem(col, 2)
@@ -43,16 +43,24 @@
         pl.semaphore_signal(barrier, inc=1, device_id=d, device_id_type=MESH)
     pl.semaphore_wait(barrier, len(peers))
 
-    sent = []
+    sent, slots, free = [], [], list(range(N_SENDS))
 
     def send(src, dst, dev):
-        k = len(sent)
+        slots.append(free.pop(free.index(min(free))))
         copy = pltpu.make_async_remote_copy(
-            src_ref=src, dst_ref=dst, send_sem=ssem.at[k], recv_sem=rsem.at[k],
+            src_ref=src, dst_ref=dst, send_sem=ssem.at[slots[-1]], recv_sem=rsem.at[len(sent)],
             device_id=dev, device_id_type=MESH)
         copy.start()
         sent.append(copy)
         return copy
+
+    done = [0]
+
+    def left(n):
+        for k in range(done[0], n):
+            sent[k].wait_send()
+            free.append(slots[k])
+        done[0] = max(done[0], n)
 
     def local(k, src, dst):
         copy = pltpu.make_async_copy(src, dst, lsem.at[k])
@@ -116,7 +124,6 @@
     b_f1 = send(grow(xl, yp, cb1), grow(xl, yp, cb1), d_ym)
     b_f0 = send(grow(xl, ym, cb0), grow(xl, ym, cb0), d_yp)
     b_x.append(send(grow(xl, ym, cb), grow(xl, ym, cb), d_xp))
-    b_x.append(send(grow(xl, yp, cb), grow(xl, yp, cb), d_xp))
     got(t_f0, t_f1)
     t_c.append(send(xrow(zb + z2), xrow(zb + z2), d_cp))
     t_c.append(send(xrow(zbx + z2), xrow(zbx + z2), d_cp))
@@ -139,74 +146,98 @@
     def prow(xx, yy):
         return pl.ds(pl.multiple_of((xx * 4 + yy) * TB, TB), TB)
 
-    def quant(rows, c0, n, q, s):
+    def scales(tile):
+        v = tile.astype(jnp.int32).astype(jnp.float32)
+        return v[8:16] * (1.0 / 8192.0) * jnp.exp2(v[0:8])
+
+    def quant(rows, c0, n, q):
         def peak(k, m):
             v = part[rows, pl.ds(pl.multiple_of(c0 + k * 128, 128), 128)]
             return jnp.maximum(m, jnp.max(jnp.abs(v.reshape(16, 8, 128)), axis=0))
 
         m = lax.fori_loop(0, n // 128, peak, jnp.full((8, 128), 1e-30, jnp.float32))
-        s[...] = m * (1.0 / 32766.0)
-        inv = 32766.0 / m
+        m = m * (1.0 / 32766.0)
+        e = jnp.floor(jnp.log2(m))
+        m = jnp.ceil(m * jnp.exp2(-e) * 8192.0)
+        tile = jnp.concatenate([e, m], axis=0).astype(jnp.int32).astype(jnp.int16)
+        q[16] = tile
+        q[33] = tile
+        inv = 1.0 / scales(tile)
 
         def code(k, carry):
             v = part[rows, pl.ds(pl.multiple_of(c0 + k * 128, 128), 128)]
-            v = (v.reshape(16, 8, 128) * inv[None]).reshape(TB, 128)
-            q[:, pl.ds(pl.multiple_of(k * 128, 128), 128)] = (
-                jnp.round(v).astype(jnp.int32).astype(jnp.int16))
+            v = (v.reshape(16, 8, 128) * inv[None]).reshape(2, 4, 16, 128)
+            v = jnp.round(v).astype(jnp.int32).astype(jnp.int16)
+            q[pl.ds(k * 4, 4)] = v[0]
+            q[pl.ds(17 + k * 4, 4)] = v[1]
             return carry
 
         lax.fori_loop(0, n // 128, code, 0)
 
-    def add(rows, c0, n, q, s):
+    def add(rows, c0, n, q):
+        s = scales(q[16])
+
         def step(k, carry):
             cols = pl.ds(pl.multiple_of(c0 + k * 128, 128), 128)
-            v = q[:, pl.ds(pl.multiple_of(k * 128, 128), 128)].astype(jnp.int32).astype(jnp.float32)
-            v = (v.reshape(16, 8, 128) * s[...][None]).reshape(TB, 128)
-            part[rows, cols] = part[rows, cols] + v
+            v = jnp.concatenate([q[pl.ds(k * 4, 4)], q[pl.ds(17 + k * 4, 4)]], axis=0)
+            v = v.astype(jnp.int32).astype(jnp.float32).reshape(16, 8, 128) * s[None]
+            part[rows, cols] = part[rows, cols] + v.reshape(TB, 128)
             return carry
 
         lax.fori_loop(0, n // 128, step, 0)
-
-    def send2(qs, ss, qr, sr, dev):
-        return send(ss, sr, dev), send(qs, qr, dev)
 
     def a_first(i):
         c0, n = A_PIECES[i]
         for yy in range(4):
-            quant(prow(xo, yy), c0, n, ax_s.at[i, yy], axs_s.at[i, yy])
-        return send2(ax_s.at[i], axs_s.at[i], ax_r.at[i], axs_r.at[i], d_xp)
+            quant(prow(xo, yy), c0, n, ax_s.at[i, yy])
+        return send(ax_s.at[i, :, pl.ds(0, 33)], ax_r.at[i, :, pl.ds(0, 33)], d_xp)
 
     def a_second(i, first):
         c0, n = A_PIECES[i]
-        yd, yo, d_d, d_o = (yp, ym, d_yp, d_ym) if i % 2 == 0 else (ym, yp, d_ym, d_yp)
-        got(*first)
+        d_d = d_yp if i % 2 == 0 else d_ym
+        got(first)
         for yy in range(4):
-            add(prow(xl, yy), c0, n, ax_r.at[i, yy], axs_r.at[i, yy])
-        far = by_y(ay_s, ay_r, ays_s, ays_r, i, 0, prow(xl, y2), c0, n, d_d)
-        near = by_y(ay_s, ay_r, ays_s, ays_r, i, 1, prow(xl, yo), c0, n, d_o)
-        return far, near
-
-    def by_y(qs, qr, ss, sr, i, k, rows, c0, n, dev):
-        quant(rows, c0, n, qs.at[i, k], ss.at[i, k])
-        return send2(qs.at[i, k], ss.at[i, k], qr.at[i, k], sr.at[i, k], dev)
+            add(prow(xl, yy), c0, n, ax_r.at[i, yy])
+        a_own.append(share(c0, n))
+        quant(prow(xl, y2), c0, n, ay_s.at[i, 0])
+        return send(ay_s.at[i, 0, pl.ds(0, 33)], ay_r.at[i, pl.ds(0, 33)], d_d)
+
+    def a_near(i):
+        c0, n = A_PIECES[i]
+        yo, d_o = (ym, d_ym) if i % 2 == 0 else (yp, d_yp)
+        quant(prow(xl, yo), c0, n, ay_s.at[i, 1])
+        return send_last(ay_s.at[i, 1], af_r.at[i, 0], d_o)
+
+    own_part = pl.ds(pl.multiple_of((xl * 4 + y) * TB + c * 64, 64), 64)
+    their_part = pl.ds(pl.multiple_of((xl * 4 + y) * TB + (1 - c) * 64, 64), 64)
+    a_own, b_own = [], []
+
+    def share(c0, n):
+        return send(part.at[their_part, pl.ds(c0, n)], oth.at[:, pl.ds(c0, n)], d_cp)
+
+    def send_last(qs, qr, dev):
+        dev2 = (dev[0], dev[1] + 1 - 2 * c)
+        return (send(qs.at[pl.ds(c * 17, 17)], qr.at[0], dev),
+                send(qs.at[pl.ds((1 - c) * 17, 17)], qr.at[1], dev2))
 
     def a_third(i, far):
         c0, n = A_PIECES[i]
         yd, d_d = (yp, d_yp) if i % 2 == 0 else (ym, d_ym)
-        got(*far)
-        add(prow(xl, yd), c0, n, ay_r.at[i, 0], ays_r.at[i, 0])
-        return by_y(ay_s, ay_r, ays_s, ays_r, i, 2, prow(xl, yd), c0, n, d_d)
+        got(far)
+        add(prow(xl, yd), c0, n, ay_r.at[i])
+        quant(prow(xl, yd), c0, n, ay_s.at[i, 2])
+        return send_last(ay_s.at[i, 2], af_r.at[i, 1], d_d)
 
     def a_last(i, near, passed):
         c0, n = A_PIECES[i]
-        got(*near, *passed)
-        add(prow(xl, y), c0, n, ay_r.at[i, 1], ays_r.at[i, 1])
-        add(prow(xl, y), c0, n, ay_r.at[i, 2], ays_r.at[i, 2])
-        finish(c0, n)
+        got(*near, *passed, a_own[i])
+        for k in range(2):
+            finish(c0, n, k, [af_r.at[i, j, k] for j in range(2)])
 
     def b_y(i, k, rows, dev):
         c0, n = B_PIECES[i]
-        return by_y(by_s, by_r, bys_s, bys_r, i, k, rows, c0, n, dev)
+        quant(rows, c0, n, by_s.at[i, k])
+        return send(by_s.at[i, k, pl.ds(0, 33)], by_r.at[i, k, pl.ds(0, 33)], dev)
 
     def b_first(i):
         return b_y(i, 0, prow(0, y2), d_yp), b_y(i, 1, prow(1, y2), d_ym)
@@ -216,30 +247,32 @@
 
     def b_second(i, first):
         c0, n = B_PIECES[i]
-        got(*first[0])
-        add(prow(0, yp), c0, n, by_r.at[i, 0], bys_r.at[i, 0])
+        got(first[0])
+        add(prow(0, yp), c0, n, by_r.at[i, 0])
         up = b_y(i, 4, prow(0, yp), d_yp)
-        got(*first[1])
-        add(prow(1, ym), c0, n, by_r.at[i, 1], bys_r.at[i, 1])
+        got(first[1])
+        add(prow(1, ym), c0, n, by_r.at[i, 1])
         down = b_y(i, 5, prow(1, ym), d_ym)
         return up, down
 
     def b_third(i, near, second):
         c0, n = B_PIECES[i]
-        got(*near[0], *near[1])
-        add(prow(1, y), c0, n, by_r.at[i, 2], bys_r.at[i, 2])
-        add(prow(0, y), c0, n, by_r.at[i, 3], bys_r.at[i, 3])
-        got(*second[0], *second[1])
-        add(prow(0, y), c0, n, by_r.at[i, 4], bys_r.at[i, 4])
-        add(prow(1, y), c0, n, by_r.at[i, 5], bys_r.at[i, 5])
-        quant(prow(xo, y), c0, n, bx_s.at[i], bxs_s.at[i])
-        return send2(bx_s.at[i], bxs_s.at[i], bx_r.at[i], bxs_r.at[i], d_xp)
+        got(*near)
+        add(prow(1, y), c0, n, by_r.at[i, 2])
+        add(prow(0, y), c0, n, by_r.at[i, 3])
+        got(*second)
+        add(prow(0, y), c0, n, by_r.at[i, 4])
+        add(prow(1, y), c0, n, by_r.at[i, 5])
+        quant(prow(xo, y), c0, n, bx_s.at[i])
+        out = send_last(bx_s.at[i], bf_r.at[i], d_xp)
+        b_own.append(share(c0, n))
+        return out
 
     def b_last(i, third):
         c0, n = B_PIECES[i]
-        got(*third)
-        add(prow(xl, y), c0, n, bx_r.at[i], bxs_r.at[i])
-        finish(c0, n)
+        got(*third, b_own[i])
+        for k in range(2):
+            finish(c0, n, k, [bf_r.at[i, k]])
 
     unit_limit = active[0] * BLOCK - row * 6144
 
@@ -256,30 +289,38 @@
 
         lax.fori_loop(lo, hi, tile, 0)
 
-    own_rows = pl.ds(pl.multiple_of(c * 64, 64), 64)
-    their_rows = pl.ds(pl.multiple_of((1 - c) * 64, 64), 64)
-    finals = []
-
-    def finish(c0, n):
-        def step(k, carry):
-            at = pl.multiple_of(c0 + k * 128, 128)
-            v = part[prow(xl, y), pl.ds(at, 128)]
+    def finish(c0, n, k, terms):
+        first = c * 3072 if k == 0 else (1 - c) * 3072
+        factors = [scales(q[16]) for q in terms]
+
+        def step(j, carry):
+            at = pl.multiple_of(c0 + j * 128, 128)
+            v = part[own_part, pl.ds(at, 128)] if k == 0 else oth[:, pl.ds(at, 128)]
+            v = v.reshape(8, 8, 128)
+            for q, s in zip(terms, factors):
+                t = q[pl.ds(j * 4, 4)].astype(jnp.int32).astype(jnp.float32)
+                v = v + t.reshape(8, 8, 128) * s[None]
+            v = v.reshape(64, 128)
             v = v * (lax.erf(v * 0.7071067811865476) + 1.0) * 0.5
-            v = jnp.where(unit_mask(c * 3072 + at, TB, 128), v, 0.0)
-            actv[:, pl.ds(at, 128)] = v.astype(jnp.bfloat16)
+            v = jnp.where(unit_mask(first + at, 64, 128), v, 0.0)
+            act[:, pl.ds(pl.multiple_of(first + at, 128), 128)] = v.astype(jnp.bfloat16)
             return carry
 
         lax.fori_loop(0, n // 128, step, 0)
-        cols = pl.ds(pl.multiple_of(c * 3072 + c0, 128), n)
-        finals.append(send(actv.at[their_rows, pl.ds(c0, n)], act.at[:, cols], d_cp))
-        act[:, cols] = actv[own_rows, pl.ds(c0, n)]
+
+    c_b1 = []
+
+    def forward(k, yy):
+        got(b_x[k])
+        c_b1.append(send(grow(xo, yy, cb), grow(xo, yy, cb), d_cp))
 
     product(0, A_COLS)
     a1 = [a_first(i) for i in range(len(A_PIECES))]
+    b_x.append(send(grow(xl, yp, cb), grow(xl, yp, cb), d_xp))
+    got(h_pp, h_pm)
+    h_f1 = send(grow(xo, yp, ca), grow(xo, yp, ca), d_ym)
     product(B_PIECES[0][0], B_PIECES[2][0])
     b1 = [b_first(0), b_first(1)]
-    got(h_pp, h_pm)
-    h_f1 = send(grow(xo, yp, ca), grow(xo, yp, ca), d_ym)
     got(p_x)
     p_pp = send(pv.at[rowx], pv.at[rowx], d_zp)
     p_pm = send(pv.at[rowx], pv.at[rowx], d_zm)
@@ -296,52 +337,58 @@
     got(b_f0)
     b_x.append(send(grow(xl, y2, cb0), grow(xl, y2, cb0), d_xp))
     l_h.wait()
-    near_rows, far_rows = pl.ds(xl * 4, 4), pl.ds(xo * 4, 4)
+    near_rows = pl.ds(xl * 4, 4)
     c_b0 = send(gs.at[near_rows, c, :, cb], gs.at[near_rows, c, :, cb], d_cp)
     got(h_f1)
     c_a = send(gs.at[:, c, :, ca], gs.at[:, c, :, ca], d_cp)
+    n1 = len(sent)
     b2 = [b_second(0, b1[0])]
+    a2 = [a_second(0, a1[0])]
     l_p.wait()
     got(p_f0, p_f1)
     pvt[...] = pv[...].reshape(1024, 768).T
     b2.append(b_second(1, b1[1]))
-    a2 = [a_second(0, a1[0])]
+    left(24)
     got(c_a)
-    grad(0, 1)
+    a2.append(a_second(1, a1[1]))
     b2.append(b_second(2, b1[2]))
-    grad(1, 2)
     b2.append(b_second(3, b1[3]))
-    grad(2, 4)
-    a2.append(a_second(1, a1[1]))
-    grad(4, 7)
+    n2 = len(sent)
+    an = [a_near(0), a_near(1)]
+    left(31)
+    grad(0, 3)
+    forward(0, y)
+    forward(1, ym)
+    grad(3, 7)
+    forward(2, yp)
+    got(b_x[3])
     b3 = [b_third(0, b1n[0], b2[0])]
-    got(*b_x)
-    c_b1 = send(gs.at[far_rows, c, :, cb], gs.at[far_rows, c, :, cb], d_cp)
+    a3 = [a_third(0, a2[0])]
+    got(b_x[4])
+    c_b1.append(send(grow(xo, y2, cb), grow(xo, y2, cb), d_cp))
     b3.append(b_third(1, b1n[1], b2[1]))
-    a3 = [a_third(0, a2[0][0])]
-    got(c_b0, c_b1)
+    a3.append(a_third(1, a2[1]))
+    got(c_b0, *c_b1)
+    left(n1)
     grad(7, 9)
     b3.append(b_third(2, b1n[2], b2[2]))
     grad(9, 10)
     b3.append(b_third(3, b1n[3], b2[3]))
-    a3.append(a_third(1, a2[1][0]))
     grad(10, 12)
+    left(n2)
     b_last(0, b3[0])
     b_last(1, b3[1])
-    a_last(0, a2[0][1], a3[0])
     b_last(2, b3[2])
+    a_last(0, an[0], a3[0])
+    a_last(1, an[1], a3[1])
     b_last(3, b3[3])
-    a_last(1, a2[1][1], a3[1])
-    got(*finals)
-    for copy in sent:
-        copy.wait_send()
+    left(len(sent))
 
 
 def exchange(active_blocks, tokens, prev_tokens, hidden_grad, weight):
     bf, f32, i16 = jnp.bfloat16, jnp.float32, jnp.int16
     any_space = pl.BlockSpec(memory_space=pl.ANY)
     vmem = pl.BlockSpec(memory_space=pltpu.VMEM)
-    na, nb = A_PIECES[0][1], B_PIECES[0][1]
     pa, pb = len(A_PIECES), len(B_PIECES)
 
     def pair(shape, dtype):
@@ -358,16 +405,15 @@
             pltpu.VMEM((768, 1024), bf),
             pltpu.VMEM((8, 2, 64, 6144), bf),
             pltpu.VMEM((1024, 3072), f32),
-            pltpu.VMEM((TB, 3072), bf),
-            *pair((pa, 4, TB, na), i16),
-            *pair((pa, 3, TB, na), i16),
-            *pair((pb, 6, TB, nb), i16),
-            *pair((pb, TB, nb), i16),
-            *pair((pa, 4, 8, 128), f32),
-            *pair((pa, 3, 8, 128), f32),
-            *pair((pb, 6, 8, 128), f32),
-            *pair((pb, 8, 128), f32),
-            pltpu.SemaphoreType.DMA((N_COPIES,)),
+            pltpu.VMEM((64, 3072), f32),
+            *pair((pa, 4, 34, 16, 128), i16),
+            pltpu.VMEM((pa, 3, 34, 16, 128), i16),
+            pltpu.VMEM((pa, 34, 16, 128), i16),
+            *pair((pb, 6, 34, 16, 128), i16),
+            pltpu.VMEM((pb, 34, 16, 128), i16),
+            pltpu.VMEM((pa, 2, 2, 17, 16, 128), i16),
+            pltpu.VMEM((pb, 2, 17, 16, 128), i16),
+            pltpu.SemaphoreType.DMA((N_SENDS,)),
             pltpu.SemaphoreType.DMA((N_COPIES,)),
             pltpu.SemaphoreType.DMA((4,)),
         ],

time: 102 us -> 99.8 us (0.978)
  Pallas kernels: 101 us -> 98.4 us
    pallas_call x1, Pallas kernels: 97.1 us -> 94.4 us  [exchange(): pl.pallas_call(kernel, out_shape=(pltpu.VMEM((64, 6144), bf), pltpu.VMEM(...]
where the time goes in v3:
time: 99.8 us; the launch traced here: 99.7 us
  Pallas kernels  98.4 us (99%)
  between operations  1.28 us (1%)
    pallas_call x1, Pallas kernels, exchange(): pl.pallas_call(kernel, out_shape=(pltpu.VMEM((64, 6144), bf), pltpu.VMEM(...  94.4 us
    pallas_call x1, Pallas kernels, store(): pl.pallas_call(store_kernel, out_shape=(jax.ShapeDtypeStruct(act.shape, a...  3.97 us

profile of v3, /device:TPU:1, one launch (start us, length us, event | category | flops | bytes accessed | tf_op | source)
XLA Modules:
  0.0 99.7 jit_solution(1562287900662363316)
XLA Ops:
  1.3 94.4 %shard_map.68 = (bf16[64,6144]{1,0:T(8,128)(2,1)S(1)}, bf16[768,6144]{1,0:T(8,128)(2,1)S(1)}) custom-call(s32[1]{0:T(128)S(6)} %copy.7.active, bf16[128,768]{1,0:T(8,128)(2,1)} %tok.1, bf16[128,768]{1,0:T(8,128)(2,1)} %prev.1, bf16[64,6144]{1,0:T(8,128)(2,1)} %hg.1, bf16[768,6144]{1,0:T(8,128)(2,1)} %w.1), custom_call_target="tpu_custom_call" | custom-call | tf_op jit(solution)/shard_map/pallas_call | solution.py:397
  95.7 4.0 %shard_map.69 = (bf16[64,6144]{1,0:T(8,128)(2,1)}, bf16[768,6144]{1,0:T(8,128)(2,1)}) custom-call(bf16[64,6144]{1,0:T(8,128)(2,1)S(1)} %get-tuple-element.4.act, bf16[768,6144]{1,0:T(8,128)(2,1)S(1)} %get-tuple-element.5.g), custom_call_target="tpu_custom_call" | custom-call | tf_op jit(solution)/shard_map/pallas_call | solution.py:438

commit v4 on v3

v4 whole, which is shorter than its diff:
```python
import jax
import jax.numpy as jnp
from jax import lax
from jax.experimental import pallas as pl
from jax.experimental.pallas import tpu as pltpu
from jax.sharding import PartitionSpec as P

BLOCK = 3072
MESH = pl.DeviceIdType.MESH
TB = 128
A_AT = (0, 512)
B_AT = (1024, 1536, 2048, 2560)
GA = 3584
GB = 1280
GSTEP = 512
N_COPIES = 81
N_SENDS = 52
VMEM_LIMIT = 54 * 1000 * 1000


def kernel(active, tok, prev, hg, w, act, g, xs, pv, pvt, gs, part, oth,
           ax_s, ax_r, ay_s, ay_r, af_s, bp_s, bp_r, bn_s, bn_r, by_s, by_r, bx_s, af_r, bf_r,
           ssem, rsem, lsem):
    row, col = lax.axis_index("row"), lax.axis_index("col")
    z, c = lax.rem(row, 4), lax.rem(col, 2)
    half = lax.div(col, 2)
    y, xl = lax.rem(half, 4), lax.div(half, 4)
    zb, yb = row - z, xl * 8 + c
    yp, ym, y2 = lax.rem(y + 1, 4), lax.rem(y + 3, 4), lax.rem(y + 2, 4)
    zp, zm, z2 = lax.rem(z + 1, 4), lax.rem(z + 3, 4), lax.rem(z + 2, 4)
    xo = 1 - xl
    rowx = lax.rem(row + 4, 8)
    zbx = rowx - z
    d_cp = (row, col + 1 - 2 * c)
    d_xp = (row, lax.rem(col + 8, 16))
    d_yp, d_ym = (row, yb + yp * 2), (row, yb + ym * 2)
    d_hx = (rowx, col)
    d_zp, d_zm = (zb + zp, col), (zb + zm, col)

    sent, slots, free = [], [], list(range(N_SENDS))

    def send(src, dst, dev):
        slots.append(free.pop(free.index(min(free))))
        copy = pltpu.make_async_remote_copy(
            src_ref=src, dst_ref=dst, send_sem=ssem.at[slots[-1]], recv_sem=rsem.at[len(sent)],
            device_id=dev, device_id_type=MESH)
        copy.start()
        sent.append(copy)
        return copy

    done = [0]

    def left(n):
        for k in range(done[0], n):
            sent[k].wait_send()
            free.append(slots[k])
        done[0] = max(done[0], n)

    def local(k, src, dst):
        copy = pltpu.make_async_copy(src, dst, lsem.at[k])
        copy.start()
        return copy

    def got(*copies):
        for copy in copies:
            copy.wait_recv()

    slab = pl.ds(pl.multiple_of(c * 768, 128), 768)
    mine = pl.ds(pl.multiple_of(c * 3072, 128), 3072)
    other = pl.ds(pl.multiple_of((1 - c) * 3072, 128), 3072)
    ca, cb = pl.ds(0, GA), pl.ds(GA, 6144 - GA)
    cb0, cb1 = pl.ds(GA, GB), pl.ds(GA + GB, 6144 - GA - GB)

    def xrow(r):
        return xs.at[r, :, slab]

    def group(r):
        return xs.at[pl.ds(r, 4), :, slab]

    def grow(xx, yy, cols):
        return gs.at[xx * 4 + yy, c, :, cols]

    l_h = local(2, hg, gs.at[xl * 4 + y, c])
    l_t = local(0, tok, xrow(row))
    l_p = local(3, prev, pv.at[row])
    l_w = local(1, w.at[:, mine], g.at[:, mine])

    barrier = pltpu.get_barrier_semaphore()
    peers = (d_cp, d_xp, d_yp, d_ym, d_hx, d_zp, d_zm)
    for d in peers:
        pl.semaphore_signal(barrier, inc=1, device_id=d, device_id_type=MESH)
    pl.semaphore_wait(barrier, len(peers))

    l_h.wait()
    l_t.wait()
    l_p.wait()
    t_x = send(xrow(row), xrow(row), d_hx)
    t_op = send(xrow(row), xrow(row), d_zp)
    t_om = send(xrow(row), xrow(row), d_zm)
    h_x = send(grow(xl, y, ca), grow(xl, y, ca), d_xp)
    h_op = send(grow(xl, y, ca), grow(xl, y, ca), d_yp)
    h_om = send(grow(xl, y, ca), grow(xl, y, ca), d_ym)
    w_c = send(w.at[:, other], g.at[:, mine], d_cp)
    b_op = send(grow(xl, y, cb), grow(xl, y, cb), d_yp)
    b_om = send(grow(xl, y, cb), grow(xl, y, cb), d_ym)
    b_x = [send(grow(xl, y, cb), grow(xl, y, cb), d_xp)]

    got(t_x)
    t_pp = send(xrow(rowx), xrow(rowx), d_zp)
    t_pm = send(xrow(rowx), xrow(rowx), d_zm)
    p_x = send(pv.at[row], pv.at[row], d_hx)
    got(t_op, t_om)
    t_f0 = send(xrow(zb + zm), xrow(zb + zm), d_zp)
    got(t_pp, t_pm)
    t_f1 = send(xrow(zbx + zp), xrow(zbx + zp), d_zm)
    p_op = send(pv.at[row], pv.at[row], d_zp)
    p_om = send(pv.at[row], pv.at[row], d_zm)
    got(h_x)
    h_pp = send(grow(xo, y, ca), grow(xo, y, ca), d_yp)
    h_pm = send(grow(xo, y, ca), grow(xo, y, ca), d_ym)
    got(h_op, h_om)
    h_f0 = send(grow(xl, ym, ca), grow(xl, ym, ca), d_yp)
    got(b_op, b_om)
    b_f1 = send(grow(xl, yp, cb1), grow(xl, yp, cb1), d_ym)
    b_f0 = send(grow(xl, ym, cb0), grow(xl, ym, cb0), d_yp)
    b_x.append(send(grow(xl, ym, cb), grow(xl, ym, cb), d_xp))
    got(t_f0, t_f1)
    t_c = [send(group(zb), group(zb), d_cp), send(group(zbx), group(zbx), d_cp)]
    l_w.wait()
    got(w_c, *t_c)

    def product(lo, hi):
        def tile(i, carry):
            cols = pl.ds(pl.multiple_of(i * 256, 256), 256)
            cols2 = pl.ds(pl.multiple_of(i * 256 + 3072, 256), 256)
            part[:, cols] = jnp.dot(
                xs[...].reshape(1024, 1536),
                jnp.concatenate([g[:, cols], g[:, cols2]], axis=0),
                preferred_element_type=jnp.float32)
            return carry

        lax.fori_loop(lo // 256, hi // 256, tile, 0)

    def prow(xx, yy):
        return pl.ds(pl.multiple_of((xx * 4 + yy) * TB, TB), TB)

    N = 512

    def scales(tile):
        v = tile.astype(jnp.int32).astype(jnp.float32)
        return v[8:16] * (1.0 / 8192.0) * jnp.exp2(v[0:8])

    def lanes(c0, k):
        return pl.ds(pl.multiple_of(c0 + k * 128, 128), 128)

    def common(blocks):
        m = jnp.full((8, 128), 1e-30, jnp.float32)
        for rows, c0 in blocks:
            def peak(k, m, rows=rows, c0=c0):
                return jnp.maximum(m, jnp.max(jnp.abs(part[rows, lanes(c0, k)].reshape(16, 8, 128)), axis=0))

            m = lax.fori_loop(0, N // 128, peak, m)
        m = m * (1.0 / 32766.0)
        e = jnp.floor(jnp.log2(m))
        m = jnp.ceil(m * jnp.exp2(-e) * 8192.0)
        tile = jnp.concatenate([e, m], axis=0).astype(jnp.int32).astype(jnp.int16)
        return tile, 1.0 / scales(tile)

    def code(rows, c0, q, inv, first=0, second=16):
        def step(k, carry):
            v = part[rows, lanes(c0, k)].reshape(16, 8, 128) * inv[None]
            v = jnp.round(v.reshape(2, 4, 16, 128)).astype(jnp.int32).astype(jnp.int16)
            q[pl.ds(first + k * 4, 4)] = v[0]
            q[pl.ds(second + k * 4, 4)] = v[1]
            return carry

        lax.fori_loop(0, N // 128, step, 0)

    def add(rows, c0, q, s, first=0):
        def step(k, carry):
            v = jnp.concatenate([q[pl.ds(first + k * 4, 4)], q[pl.ds(first + 16 + k * 4, 4)]], axis=0)
            v = v.astype(jnp.int32).astype(jnp.float32).reshape(16, 8, 128) * s[None]
            part[rows, lanes(c0, k)] = part[rows, lanes(c0, k)] + v.reshape(TB, 128)
            return carry

        lax.fori_loop(0, N // 128, step, 0)

    def post(rows, c0, qs, qr, dev):
        tile, inv = common([(rows, c0)])
        code(rows, c0, qs, inv)
        qs[32] = tile
        return send(qs, qr, dev)

    def post_last(rows, c0, qs, qr, dev):
        tile, inv = common([(rows, c0)])
        code(rows, c0, qs, inv, 0, 17)
        qs[16] = tile
        qs[33] = tile
        dev2 = (dev[0], dev[1] + 1 - 2 * c)
        return (send(qs.at[pl.ds(c * 17, 17)], qr.at[0], dev),
                send(qs.at[pl.ds((1 - c) * 17, 17)], qr.at[1], dev2))

    own_part = pl.ds(pl.multiple_of((xl * 4 + y) * TB + c * 64, 64), 64)
    their_part = pl.ds(pl.multiple_of((xl * 4 + y) * TB + (1 - c) * 64, 64), 64)
    a_own, b_own = [], []

    def share(c0):
        return send(part.at[their_part, pl.ds(c0, N)], oth.at[:, pl.ds(c0, N)], d_cp)

    def a_first(i):
        blocks = [(prow(xo, yy), A_AT[i]) for yy in range(4)]
        tile, inv = common(blocks)
        for yy, (rows, c0) in enumerate(blocks):
            code(rows, c0, ax_s.at[i], inv, yy * 32, yy * 32 + 16)
        ax_s[i, 128] = tile
        return send(ax_s.at[i], ax_r.at[i], d_xp)

    def a_second(i, first):
        c0 = A_AT[i]
        got(first)
        s = scales(ax_r[i, 128])
        for yy in range(4):
            add(prow(xl, yy), c0, ax_r.at[i], s, yy * 32)
        a_own.append(share(c0))
        return post(prow(xl, y2), c0, ay_s.at[i], ay_r.at[i], d_yp if i % 2 == 0 else d_ym)

    def a_near(i):
        yo, d_o = (ym, d_ym) if i % 2 == 0 else (yp, d_yp)
        return post_last(prow(xl, yo), A_AT[i], af_s.at[i, 0], af_r.at[i, 0], d_o)

    def a_third(i, far):
        yd, d_d = (yp, d_yp) if i % 2 == 0 else (ym, d_ym)
        got(far)
        add(prow(xl, yd), A_AT[i], ay_r.at[i], scales(ay_r[i, 32]))
        return post_last(prow(xl, yd), A_AT[i], af_s.at[i, 1], af_r.at[i, 1], d_d)

    def a_last(i, near, passed):
        got(*near, *passed, a_own[i])
        for k in range(2):
            finish(A_AT[i], k, [af_r.at[i, j, k] for j in range(2)])

    def b_first(p):
        out = []
        for k, far_rows, near_rows, dev in ((0, prow(0, y2), prow(1, yp), d_yp), (1, prow(1, y2), prow(0, ym), d_ym)):
            at = [B_AT[2 * p], B_AT[2 * p + 1]]
            tile, inv = common([(r, c0) for r in (far_rows, near_rows) for c0 in at])
            for j in range(2):
                code(far_rows, at[j], bp_s.at[p, k], inv, j * 32, j * 32 + 16)
                code(near_rows, at[j], bn_s.at[p, k], inv, j * 32, j * 32 + 16)
            bp_s[p, k, 64] = tile
            out.append(send(bp_s.at[p, k], bp_r.at[p, k], dev))
        return out

    def b_near(p):
        return [send(bn_s.at[p, k], bn_r.at[p, k], dev) for k, dev in ((0, d_yp), (1, d_ym))]

    def b_second(i, first):
        p, j, out = i // 2, i % 2, []
        for k, rows, dev in ((0, prow(0, yp), d_yp), (1, prow(1, ym), d_ym)):
            if j == 0:
                got(first[k])
            add(rows, B_AT[i], bp_r.at[p, k], scales(bp_r[p, k, 64]), j * 32)
            out.append(post(rows, B_AT[i], by_s.at[i, k], by_r.at[i, k], dev))
        return out

    def b_third(i, near, second):
        p, j, c0 = i // 2, i % 2, B_AT[i]
        if j == 0:
            got(*near)
        for k, rows in ((0, prow(1, y)), (1, prow(0, y))):
            add(rows, c0, bn_r.at[p, k], scales(bp_r[p, k, 64]), j * 32)
        got(*second)
        for k, rows in ((0, prow(0, y)), (1, prow(1, y))):
            add(rows, c0, by_r.at[i, k], scales(by_r[i, k, 32]))
        out = post_last(prow(xo, y), c0, bx_s.at[i], bf_r.at[i], d_xp)
        b_own.append(share(c0))
        return out

    def b_last(i, third):
        got(*third, b_own[i])
        for k in range(2):
            finish(B_AT[i], k, [bf_r.at[i, k]])

    unit_limit = active[0] * BLOCK - row * 6144

    def unit_mask(first, rows, n):
        return first + lax.broadcasted_iota(jnp.int32, (rows, n), 1) < unit_limit

    def grad(lo, hi):
        def tile(i, carry):
            cols = pl.ds(pl.multiple_of(i * GSTEP, GSTEP), GSTEP)
            v = jnp.dot(pvt[...], gs[:, :, :, cols].reshape(1024, GSTEP),
                        preferred_element_type=jnp.float32)
            g[:, cols] = jnp.where(unit_mask(i * GSTEP, 768, GSTEP), v, 0.0).astype(jnp.bfloat16)
            return carry

        lax.fori_loop(lo, hi, tile, 0)

    def finish(c0, k, terms):
        first = c * 3072 if k == 0 else (1 - c) * 3072
        factors = [scales(q[16]) for q in terms]

        def step(j, carry):
            at = pl.multiple_of(c0 + j * 128, 128)
            v = part[own_part, pl.ds(at, 128)] if k == 0 else oth[:, pl.ds(at, 128)]
            v = v.reshape(8, 8, 128)
            for q, s in zip(terms, factors):
                t = q[pl.ds(j * 4, 4)].astype(jnp.int32).astype(jnp.float32)
                v = v + t.reshape(8, 8, 128) * s[None]
            v = v.reshape(64, 128)
            v = v * (lax.erf(v * 0.7071067811865476) + 1.0) * 0.5
            v = jnp.where(unit_mask(first + at, 64, 128), v, 0.0)
            act[:, pl.ds(pl.multiple_of(first + at, 128), 128)] = v.astype(jnp.bfloat16)
            return carry

        lax.fori_loop(0, N // 128, step, 0)

    c_b1 = []

    def forward(k, yy):
        got(b_x[k])
        c_b1.append(send(grow(xo, yy, cb), grow(xo, yy, cb), d_cp))

    product(0, 1024)
    a1 = [a_first(i) for i in range(2)]
    b_x.append(send(grow(xl, yp, cb), grow(xl, yp, cb), d_xp))
    got(h_pp, h_pm)
    h_f1 = send(grow(xo, yp, ca), grow(xo, yp, ca), d_ym)
    product(1024, 2048)
    b1 = [b_first(0)]
    got(p_x)
    p_pp = send(pv.at[rowx], pv.at[rowx], d_zp)
    p_pm = send(pv.at[rowx], pv.at[rowx], d_zm)
    got(b_f1)
    b_x.append(send(grow(xl, y2, cb1), grow(xl, y2, cb1), d_xp))
    product(2048, 3072)
    b1.append(b_first(1))
    got(p_op, p_om)
    p_f0 = send(pv.at[zb + zm], pv.at[zb + zm], d_zp)
    b1n = [b_near(0)]
    got(p_pp, p_pm)
    p_f1 = send(pv.at[zbx + zp], pv.at[zbx + zp], d_zm)
    got(h_f0)
    got(b_f0)
    b_x.append(send(grow(xl, y2, cb0), grow(xl, y2, cb0), d_xp))
    near_rows = pl.ds(xl * 4, 4)
    c_b0 = send(gs.at[near_rows, c, :, cb], gs.at[near_rows, c, :, cb], d_cp)
    got(h_f1)
    c_a = send(gs.at[:, c, :, ca], gs.at[:, c, :, ca], d_cp)
    n1 = len(sent)
    b2 = [b_second(0, b1[0])]
    b1n.append(b_near(1))
    a2 = [a_second(0, a1[0])]
    got(p_f0, p_f1)
    pvt[...] = pv[...].reshape(1024, 768).T
    b2.append(b_second(1, b1[0]))
    left(19)
    b2.append(b_second(2, b1[1]))
    b2.append(b_second(3, b1[1]))
    n2 = len(sent)
    got(c_a)
    grad(0, 2)
    a2.append(a_second(1, a1[1]))
    an = [a_near(0), a_near(1)]
    forward(0, y)
    forward(1, ym)
    grad(2, 3)
    b3 = [b_third(0, b1n[0], b2[0])]
    left(24)
    grad(3, 5)
    forward(2, yp)
    a3 = [a_third(0, a2[0])]
    grad(5, 6)
    b3.append(b_third(1, b1n[0], b2[1]))
    got(b_x[3], b_x[4])
    c_b1.append(send(grow(xo, y2, cb), grow(xo, y2, cb), d_cp))
    b3.append(b_third(2, b1n[1], b2[2]))
    left(n1)
    got(c_b0, *c_b1)
    grad(6, 8)
    a3.append(a_third(1, a2[1]))
    b3.append(b_third(3, b1n[1], b2[3]))
    grad(8, 12)
    left(n2)
    b_last(0, b3[0])
    b_last(1, b3[1])
    b_last(2, b3[2])
    b_last(3, b3[3])
    a_last(0, an[0], a3[0])
    a_last(1, an[1], a3[1])
    left(len(sent))


def exchange(active_blocks, tokens, prev_tokens, hidden_grad, weight):
    bf, f32, i16 = jnp.bfloat16, jnp.float32, jnp.int16
    any_space = pl.BlockSpec(memory_space=pl.ANY)
    vmem = pl.BlockSpec(memory_space=pltpu.VMEM)
    pa, pb = len(A_AT), len(B_AT)

    def pair(shape, dtype):
        return [pltpu.VMEM(shape, dtype)] * 2

    return pl.pallas_call(
        kernel,
        out_shape=(pltpu.VMEM((64, 6144), bf), pltpu.VMEM((768, 6144), bf)),
        in_specs=[pl.BlockSpec(memory_space=pltpu.SMEM)] + [any_space] * 4,
        out_specs=(vmem, vmem),
        scratch_shapes=[
            pltpu.VMEM((8, 128, 1536), bf),
            pltpu.VMEM((8, 128, 768), bf),
            pltpu.VMEM((768, 1024), bf),
            pltpu.VMEM((8, 2, 64, 6144), bf),
            pltpu.VMEM((1024, 3072), f32),
            pltpu.VMEM((64, 3072), f32),
            *pair((pa, 129, 16, 128), i16),
            *pair((pa, 33, 16, 128), i16),
            pltpu.VMEM((pa, 2, 34, 16, 128), i16),
            *pair((pb // 2, 2, 65, 16, 128), i16),
            *pair((pb // 2, 2, 64, 16, 128), i16),
            *pair((pb, 2, 33, 16, 128), i16),
            pltpu.VMEM((pb, 34, 16, 128), i16),
            pltpu.VMEM((pa, 2, 2, 17, 16, 128), i16),
            pltpu.VMEM((pb, 2, 17, 16, 128), i16),
            pltpu.SemaphoreType.DMA((N_SENDS,)),
            pltpu.SemaphoreType.DMA((N_COPIES,)),
            pltpu.SemaphoreType.DMA((4,)),
        ],
        compiler_params=pltpu.CompilerParams(
            collective_id=0, has_side_effects=True, vmem_limit_bytes=VMEM_LIMIT),
    )(active_blocks, *(pltpu.with_memory_space_constraint(a, pltpu.HBM)
                       for a in (tokens, prev_tokens, hidden_grad, weight)))


def store_kernel(act, g, act_out, g_out, sems):
    copies = [pltpu.make_async_copy(act, act_out, sems.at[8])]
    for k in range(8):
        rows = pl.ds(k * 96, 96)
        copies.append(pltpu.make_async_copy(g.at[rows], g_out.at[rows], sems.at[k]))
    for copy in copies:
        copy.start()
    for copy in copies:
        copy.wait()


def store(act, g):
    return pl.pallas_call(
        store_kernel,
        out_shape=(jax.ShapeDtypeStruct(act.shape, act.dtype), jax.ShapeDtypeStruct(g.shape, g.dtype)),
        in_specs=[pl.BlockSpec(memory_space=pltpu.VMEM)] * 2,
        out_specs=[pl.BlockSpec(memory_space=pl.ANY)] * 2,
        scratch_shapes=[pltpu.SemaphoreType.DMA((9,))],
        compiler_params=pltpu.CompilerParams(vmem_limit_bytes=12 * 1024 * 1024),
    )(act, g)


def shards(tokens, prev_tokens, hidden_grad, active_blocks, weight):
    act, grad = exchange(active_blocks, tokens, prev_tokens, hidden_grad, weight)
    return tuple(store(act, grad))


def solution(mesh):
    return jax.shard_map(
        shards,
        mesh=mesh,
        in_specs=(P("row", "col"), P("row", "col"), P("col", "row"), P(), P("col", "row")),
        out_specs=(P("col", "row"), P("col", "row")),
        check_vma=False,
    )
```

time: 99.8 us -> 98.9 us (level)
  no operation moved by 1% of the time
where the time goes in v4:
time: 98.9 us; the launch traced here: 98.8 us
  Pallas kernels  97.5 us (99%)
  between operations  1.28 us (1%)
    pallas_call x1, Pallas kernels, exchange(): pl.pallas_call(kernel, out_shape=(pltpu.VMEM((64, 6144), bf), pltpu.VMEM(...  93.6 us
    pallas_call x1, Pallas kernels, store(): pl.pallas_call(store_kernel, out_shape=(jax.ShapeDtypeStruct(act.shape, a...  3.94 us

profile of v4, /device:TPU:1, one launch (start us, length us, event | category | flops | bytes accessed | tf_op | source)
XLA Modules:
  0.0 98.8 jit_solution(2118885524674611936)
XLA Ops:
  1.3 93.6 %shard_map.68 = (bf16[64,6144]{1,0:T(8,128)(2,1)S(1)}, bf16[768,6144]{1,0:T(8,128)(2,1)S(1)}) custom-call(s32[1]{0:T(128)S(6)} %copy.7.active, bf16[128,768]{1,0:T(8,128)(2,1)} %tok.1, bf16[128,768]{1,0:T(8,128)(2,1)} %prev.1, bf16[64,6144]{1,0:T(8,128)(2,1)} %hg.1, bf16[768,6144]{1,0:T(8,128)(2,1)} %w.1), custom_call_target="tpu_custom_call" | custom-call | tf_op jit(solution)/shard_map/pallas_call | solution.py:403
  94.9 3.9 %shard_map.69 = (bf16[64,6144]{1,0:T(8,128)(2,1)}, bf16[768,6144]{1,0:T(8,128)(2,1)}) custom-call(bf16[64,6144]{1,0:T(8,128)(2,1)S(1)} %get-tuple-element.4.act, bf16[768,6144]{1,0:T(8,128)(2,1)S(1)} %get-tuple-element.5.g), custom_call_target="tpu_custom_call" | custom-call | tf_op jit(solution)/shard_map/pallas_call | solution.py:446

commit v5 on v4

--- a/solution.py
+++ b/solution.py
@@ -14,7 +14,7 @@
 GB = 1280
 GSTEP = 512
 N_COPIES = 81
-N_SENDS = 52
+N_SENDS = 51
 VMEM_LIMIT = 54 * 1000 * 1000
 
 
@@ -369,25 +369,26 @@
     left(24)
     grad(3, 5)
     forward(2, yp)
-    a3 = [a_third(0, a2[0])]
     grad(5, 6)
-    b3.append(b_third(1, b1n[0], b2[1]))
     got(b_x[3], b_x[4])
     c_b1.append(send(grow(xo, y2, cb), grow(xo, y2, cb), d_cp))
-    b3.append(b_third(2, b1n[1], b2[2]))
+    a3 = [a_third(0, a2[0])]
+    b3.append(b_third(1, b1n[0], b2[1]))
     left(n1)
     got(c_b0, *c_b1)
     grad(6, 8)
+    b3.append(b_third(2, b1n[1], b2[2]))
+    grad(8, 10)
+    b3.append(b_third(3, b1n[1], b2[3]))
     a3.append(a_third(1, a2[1]))
-    b3.append(b_third(3, b1n[1], b2[3]))
-    grad(8, 12)
+    grad(10, 12)
     left(n2)
     b_last(0, b3[0])
     b_last(1, b3[1])
     b_last(2, b3[2])
-    b_last(3, b3[3])
     a_last(0, an[0], a3[0])
     a_last(1, an[1], a3[1])
+    b_last(3, b3[3])
     left(len(sent))
 
 

time: 98.9 us -> 98.8 us (level)
  no operation moved by 1% of the time
where the time goes in v5:
time: 98.8 us; the launch traced here: 98.7 us
  Pallas kernels  97.4 us (99%)
  between operations  1.28 us (1%)
    pallas_call x1, Pallas kernels, exchange(): pl.pallas_call(kernel, out_shape=(pltpu.VMEM((64, 6144), bf), pltpu.VMEM(...  93.4 us
    pallas_call x1, Pallas kernels, store(): pl.pallas_call(store_kernel, out_shape=(jax.ShapeDtypeStruct(act.shape, a...  3.94 us

profile of v5, /device:TPU:1, one launch (start us, length us, event | category | flops | bytes accessed | tf_op | source)
XLA Modules:
  0.0 98.7 jit_solution(9804255837115886173)
XLA Ops:
  1.3 93.4 %shard_map.68 = (bf16[64,6144]{1,0:T(8,128)(2,1)S(1)}, bf16[768,6144]{1,0:T(8,128)(2,1)S(1)}) custom-call(s32[1]{0:T(128)S(6)} %copy.7.active, bf16[128,768]{1,0:T(8,128)(2,1)} %tok.1, bf16[128,768]{1,0:T(8,128)(2,1)} %prev.1, bf16[64,6144]{1,0:T(8,128)(2,1)} %hg.1, bf16[768,6144]{1,0:T(8,128)(2,1)} %w.1), custom_call_target="tpu_custom_call" | custom-call | tf_op jit(solution)/shard_map/pallas_call | solution.py:404
  94.7 3.9 %shard_map.69 = (bf16[64,6144]{1,0:T(8,128)(2,1)}, bf16[768,6144]{1,0:T(8,128)(2,1)}) custom-call(bf16[64,6144]{1,0:T(8,128)(2,1)S(1)} %get-tuple-element.4.act, bf16[768,6144]{1,0:T(8,128)(2,1)S(1)} %get-tuple-element.5.g), custom_call_target="tpu_custom_call" | custom-call | tf_op jit(solution)/shard_map/pallas_call | solution.py:447
